TPU v7x, 8 devices: a whole 2x2x1 slice. The times are simulated.
8 devices in a mesh: dp: 2 (over z, y), sp: 4 (over x, core).
Axes of the slice: x: 2, y: 2, z: 1, core: 2. Of those that a mesh axis runs over, the one named last changes fastest.
Arguments:
- x_rows: bfloat16 [16384, 384], P(('dp', 'sp')), parts along dimension 0
- dy_rows: bfloat16 [16384, 384], P(('dp', 'sp')), parts along dimension 0
- ln_gamma: float32 [384], replicated
- ln_beta: float32 [384], replicated
- w_qkv: bfloat16 [384, 1152], replicated
- w_out: bfloat16 [384, 384], replicated
- temperature: float32 [8], replicated
Outputs:
- output 1: bfloat16 [16384, 384], P(('dp', 'sp')), parts along dimension 0
- output 2: bfloat16 [16384, 384], P(('dp', 'sp')), parts along dimension 0
- output 3: bfloat16 [768, 1152], P(('dp', 'sp')), parts along dimension 0
- output 4: bfloat16 [768, 384], P(('dp', 'sp')), parts along dimension 0
- output 5: float32 [768], P('dp'), parts along dimension 0
- output 6: float32 [768], P('dp'), parts along dimension 0
- output 7: float32 [16], P('dp'), parts along dimension 0
There are 2 independent parts. A program takes and returns all parts, laid end to end along the dimension named above; an argument that names none is the same for every part.
All inputs are finite; a program needn't handle non-finite values.
Results may differ from a plain program's by a relative error of at most 0.0120056.
Values are sent between devices in bfloat16 or wider.
A program may use at most 1 GiB of HBM per device.

v0:
```python
import jax
import jax.numpy as jnp
from jax import lax
from jax.sharding import PartitionSpec as P

LN_EPS = 1e-6


def layer_norm_fwd(x_rows, ln_gamma, ln_beta):
    x_f32 = x_rows.astype(jnp.float32)
    centered = x_f32 - jnp.mean(x_f32, axis=-1, keepdims=True)
    inv_std = lax.rsqrt(jnp.mean(centered * centered, axis=-1, keepdims=True) + LN_EPS)
    x_hat = centered * inv_std
    normed = (x_hat * ln_gamma + ln_beta).astype(jnp.bfloat16)
    return normed, x_hat, inv_std


def layer_norm_bwd(d_normed, x_hat, inv_std, ln_gamma):
    d_f32 = d_normed.astype(jnp.float32)
    d_gamma_part = jnp.sum(d_f32 * x_hat, axis=0)
    d_beta_part = jnp.sum(d_f32, axis=0)
    d_hat = d_f32 * ln_gamma
    d_x = inv_std * (d_hat - jnp.mean(d_hat, axis=-1, keepdims=True) - x_hat * jnp.mean(d_hat * x_hat, axis=-1, keepdims=True))
    return d_x, d_gamma_part, d_beta_part


def state_softmax(gram, q_sq, k_sq, value_a11):
    q_inv = lax.rsqrt(q_sq)[:, :, None]
    k_inv = lax.rsqrt(k_sq)[:, None, :]
    scores = value_a11[:, None, None] * gram * q_inv * k_inv
    return jax.nn.softmax(scores, axis=-1), scores


def state_softmax_bwd(d_attn, attn_f32, scores, gram, q_sq, k_sq, value_a11):
    d_scores = attn_f32 * (d_attn - jnp.sum(d_attn * attn_f32, axis=-1, keepdims=True))
    q_inv = lax.rsqrt(q_sq)[:, :, None]
    k_inv = lax.rsqrt(k_sq)[:, None, :]
    d_temp = jnp.sum(d_scores * gram * q_inv * k_inv, axis=(1, 2))
    d_gram = (d_scores * value_a11[:, None, None] * q_inv * k_inv).astype(jnp.bfloat16)
    weighted = d_scores * scores
    d_q_sq = -0.5 * jnp.sum(weighted, axis=2) / q_sq
    d_k_sq = -0.5 * jnp.sum(weighted, axis=1) / k_sq
    return d_gram, d_q_sq, d_k_sq, d_temp


def xca_local(x_rows, dy_rows, ln_gamma, ln_beta, w_qkv, w_out, value_a11):
    n_local, model_width = x_rows.shape
    n_heads = value_a11.shape[0]
    head_dim = model_width // n_heads
    normed, x_hat, inv_std = layer_norm_fwd(x_rows, ln_gamma, ln_beta)
    qkv_all = jnp.dot(normed, w_qkv, preferred_element_type=jnp.float32).astype(jnp.bfloat16)
    qkv_heads = qkv_all.reshape(n_local, 3, n_heads, head_dim)
    query_h = qkv_heads[:, 0]
    key_h = qkv_heads[:, 1]
    value_h = qkv_heads[:, 2]
    gram_part = jnp.einsum('nhi,nhj->hij', query_h, key_h, preferred_element_type=jnp.float32)
    q_sq_part = jnp.sum(jnp.square(query_h.astype(jnp.float32)), axis=0)
    k_sq_part = jnp.sum(jnp.square(key_h.astype(jnp.float32)), axis=0)
    gram, q_sq, k_sq = lax.psum((gram_part, q_sq_part, k_sq_part), 'sp')
    attn_f32, scores = state_softmax(gram, q_sq, k_sq, value_a11)
    attn = attn_f32.astype(jnp.bfloat16)
    attn_out = jnp.einsum('nhj,hij->nhi', value_h, attn, preferred_element_type=jnp.float32).astype(jnp.bfloat16)
    out_flat = attn_out.reshape(n_local, model_width)
    y_rows = (x_rows.astype(jnp.float32) + jnp.dot(out_flat, w_out, preferred_element_type=jnp.float32)).astype(jnp.bfloat16)

    d_out = jnp.einsum('nc,dc->nd', dy_rows, w_out, preferred_element_type=jnp.float32).astype(jnp.bfloat16)
    dw_out_part = jnp.einsum('nd,nc->dc', out_flat, dy_rows, preferred_element_type=jnp.float32)
    d_out_h = d_out.reshape(n_local, n_heads, head_dim)
    d_attn_part = jnp.einsum('nhi,nhj->hij', d_out_h, value_h, preferred_element_type=jnp.float32)
    d_attn = lax.psum(d_attn_part, 'sp').astype(jnp.bfloat16).astype(jnp.float32)
    d_gram, d_q_sq, d_k_sq, d_temp = state_softmax_bwd(d_attn, attn_f32, scores, gram, q_sq, k_sq, value_a11)
    d_query = jnp.einsum('hij,nhj->nhi', d_gram, key_h, preferred_element_type=jnp.float32) + 2.0 * query_h.astype(jnp.float32) * d_q_sq
    d_key = jnp.einsum('hij,nhi->nhj', d_gram, query_h, preferred_element_type=jnp.float32) + 2.0 * key_h.astype(jnp.float32) * d_k_sq
    d_value = jnp.einsum('nhi,hij->nhj', d_out_h, attn, preferred_element_type=jnp.float32)
    d_qkv = jnp.stack([d_query, d_key, d_value], axis=1).astype(jnp.bfloat16).reshape(n_local, 3 * model_width)
    d_normed = jnp.einsum('nc,dc->nd', d_qkv, w_qkv, preferred_element_type=jnp.float32).astype(jnp.bfloat16)
    dw_qkv_part = jnp.einsum('nd,nc->dc', normed, d_qkv, preferred_element_type=jnp.float32)
    d_ln, d_gamma_part, d_beta_part = layer_norm_bwd(d_normed, x_hat, inv_std, ln_gamma)
    dx_rows = (dy_rows.astype(jnp.float32) + d_ln).astype(jnp.bfloat16)
    dw_qkv = lax.psum_scatter(dw_qkv_part, 'sp', scatter_dimension=0, tiled=True).astype(jnp.bfloat16)
    dw_out = lax.psum_scatter(dw_out_part, 'sp', scatter_dimension=0, tiled=True).astype(jnp.bfloat16)
    d_gamma, d_beta = lax.psum((d_gamma_part, d_beta_part), 'sp')
    return y_rows, dx_rows, dw_qkv, dw_out, d_gamma, d_beta, d_temp


def solution(mesh):
    row_spec = P(('dp', 'sp'), None)
    full_mat = P(None, None)
    full_vec = P(None)
    part_vec = P('dp')
    return jax.shard_map(xca_local, mesh=mesh, in_specs=(row_spec, row_spec, full_vec, full_vec, full_mat, full_mat, full_vec), out_specs=(row_spec, row_spec, row_spec, row_spec, part_vec, part_vec, part_vec), check_vma=False)
```

profile of v0, /device:TPU:0, one launch (start us, length us, event | category | flops | bytes accessed | tf_op | source)
XLA Modules:
  0.0 116.6 jit_solution(10831897051086722661)
XLA Ops:
  7.2 0.0 all-reduce.4.cloned.1.call-start
  7.3 1.9 %convert_reduce_fusion.1 = f32[2048]{0:T(1024)S(1)} fusion(bf16[2048,384]{1,0:T(8,128)(2,1)} %param.7), kind=kLoop, calls=%fused_computation.8 | loop fusion | flops 1570816 | bytes 1581056 | tf_op jit(solution)/shard_map/reduce_sum | solution.py:11
  9.2 2.2 %fusion.15 = f32[2048]{0:T(1024)S(1)} fusion(bf16[2048,384]{1,0:T(8,128)(2,1)} %param.7, f32[2048]{0:T(1024)S(1)} %broadcast_multiply_fusion.2), kind=kLoop, calls=%fused_computation.27 | loop fusion | flops 3143680 | bytes 1589248 | tf_op jit(solution)/shard_map/reduce_sum | solution.py:12
  11.4 3.4 %convolution_convert_fusion = bf16[2048,1152]{0,1:T(8,128)(2,1)S(1)} fusion(bf16[384,1152]{1,0:T(8,128)(2,1)S(1)} %copy-done, bf16[2048,384]{1,0:T(8,128)(2,1)S(1)} %copy-done.1, f32[384]{0:T(512)S(1)} %copy-done.12, f32[384]{0:T(512)S(1)} %copy-done.11, f32[2048]{0:T(1024)S(1)} %add_rsqrt_fusion, f32[2048]{0:T(1024)S(1)} %broadcast_multiply_fusion.2), kind=kOutput, calls=%fused_computation.2 | convolution fusion | flops 1819017216 | bytes 7195648 | tf_op jit(solution)/shard_map/dot_general | solution.py:51
  14.8 2.1 %copy-done.4 = bf16[2048,1152]{0,1:T(8,128)(2,1)} copy-done((bf16[2048,1152]{0,1:T(8,128)(2,1)}, bf16[2048,1152]{0,1:T(8,128)(2,1)S(1)}, u32[]{:S(2)}) %copy-start.4) | copy-done | bytes 4718616
  16.9 1.2 %fusion.33 = f32[8,48,48]{2,1,0:T(8,128)} fusion(bf16[2048,3,8,48]{0,3,2,1:T(8,128)(2,1)S(1)} %bitcast.56), kind=kOutput, calls=%fused_computation.52 | convolution fusion | flops 75497472 | bytes 3219456 | tf_op jit(solution)/shard_map/nhi,nhj->hij/dot_general | solution.py:56
  18.2 0.0 all-reduce.4.cloned.1.call-update
  18.2 0.0 reduce-scatter.5.cloned.1.call-start
  18.3 2.6 %convolution_convert_fusion.3 = bf16[2048,384]{0,1:T(8,128)(2,1)S(1)} fusion(bf16[2048,384]{1,0:T(8,128)(2,1)} %param.8, bf16[384,384]{1,0:T(8,128)(2,1)S(1)} %copy-done.9), kind=kOutput, calls=%fused_computation.39 | convolution fusion | flops 604766208 | bytes 3440640 | tf_op jit(solution)/shard_map/nc,dc->nd/dot_general | solution.py:66
  20.8 1.1 copy-done.3
  22.0 0.7 fusion.28
  22.7 0.7 fusion.16
  23.4 16.4 %all-reduce.1 = (f32[8,48]{1,0:T(8,128)S(1)}, f32[8,48]{1,0:T(8,128)S(1)}, bf16[8,48,48]{2,1,0:T(8,128)(2,1)S(1)}) all-reduce(f32[8,48]{1,0:T(8,128)S(1)} %get-tuple-element.8, f32[8,48]{1,0:T(8,128)S(1)} %get-tuple-element.7, f32[8,48,48]{2,1,0:T(8,128)S(1)} %fusion.28), channel_id=1, replica_groups=mesh['dp'=2,'sp'=4] {'sp'}, use_global_device_ids=true, to_apply=%region_6.0 | all-reduce | flops 19200 | bytes 116736 | tf_op jit(solution)/shard_map/psum | solution.py:59
  39.8 7.9 %all-reduce.4.cloned.1.call-done = f32[8,48,48]{2,1,0:T(8,128)} async-done(((f32[8,48,48]{2,1,0:T(8,128)}), f32[8,48,48]{2,1,0:T(8,128)}) %all-reduce.4.cloned.1.call-update) | async-done | bytes 73744 | tf_op jit(solution)/shard_map/psum | solution.py:59
  47.7 2.3 %fusion.48 = (f32[8,48]{1,0:T(8,128)S(1)}, f32[8,48,48]{2,1,0:T(8,128)S(1)}) fusion(f32[8,48,48]{2,1,0:T(8,128)} %all-reduce.4.cloned.1.call-done, f32[8,48]{1,0:T(8,128)S(1)} %rsqrt.18, f32[8,48]{1,0:T(8,128)S(1)} %rsqrt.17, f32[8]{0:T(128)S(1)} %copy-done.10), kind=kOutput, calls=%fused_computation.76 | output fusion | flops 92207 | bytes 152096 | tf_op jit(solution)/shard_map/sub | solution.py:31
  50.0 4.2 %convolution_convert_fusion.4 = bf16[8,48,2048]{2,1,0:T(8,128)(2,1)} fusion(bf16[2048,3,8,48]{0,3,2,1:T(8,128)(2,1)} %bitcast.57, f32[8,48]{1,0:T(8,128)S(1)} %get-tuple-element.21, f32[8,48,48]{2,1,0:T(8,128)} %all-reduce.4.cloned.1.call-done, f32[8,48]{1,0:T(8,128)S(1)} %rsqrt.18, f32[8,48]{1,0:T(8,128)S(1)} %rsqrt.17, f32[8]{0:T(128)S(1)} %copy-done.10), kind=kOutput, calls=%fused_computation.40 | convolution fusion | flops 76394928 | bytes 3346976 | tf_op jit(solution)/shard_map/nhj,hij->nhi/dot_general | solution.py:62
  54.2 3.8 %fusion.49 = f32[384,384]{1,0:T(8,128)} fusion(bf16[2048,384]{0,1:T(8,128)(2,1)} %bitcast.64, bf16[2048,384]{1,0:T(8,128)(2,1)} %param.8), kind=kOutput, calls=%fused_computation.77 | convolution fusion | flops 603979776 | bytes 3735552 | tf_op jit(solution)/shard_map/nd,nc->dc/dot_general | solution.py:67
  58.0 0.2 reduce-scatter.3.cloned.1.call-start
  58.2 2.6 %fusion.44 = (f32[8,48]{1,0:T(8,128)S(1)}, f32[8,48]{1,0:T(8,128)S(1)}, f32[8]{0:T(128)}) fusion(f32[8,48]{1,0:T(8,128)S(1)} %rsqrt.18, f32[8,48]{1,0:T(8,128)S(1)} %rsqrt.17, f32[8,48,48]{2,1,0:T(8,128)S(1)} %copy-done.8, f32[8]{0:T(128)S(1)} %copy-done.10, bf16[8,48,48]{2,1,0:T(8,128)(2,1)S(1)} %get-tuple-element.20, ...), kind=kOutput, calls=%fused_computation.74 | output fusion | flops 312999 | bytes 192064 | tf_op jit(solution)/shard_map/sub | solution.py:35
  60.9 5.4 %fusion.26 = bf16[2048,1,8,48]{0,3,2,1:T(8,128)(2,1)} fusion(f32[8,48]{1,0:T(8,128)S(1)} %get-tuple-element.24, bf16[2048,3,8,48]{0,3,2,1:T(8,128)(2,1)} %bitcast.58, f32[8,48]{1,0:T(8,128)S(1)} %rsqrt.18, f32[8,48]{1,0:T(8,128)S(1)} %rsqrt.17, f32[8]{0:T(128)S(1)} %copy-done.10, bf16[8,48,48]{2,1,0:T(8,128)(2,1)S(1)} %get-tuple-element.20, ...), kind=kOutput, calls=%fused_computation.42 | convolution fusion | flops 78846384 | bytes 5329408 | tf_op jit(solution)/shard_map/hij,nhi->nhj/dot_general | solution.py:73
  66.3 5.1 %fusion.27 = bf16[2048,1,8,48]{0,3,2,1:T(8,128)(2,1)} fusion(f32[8,48]{1,0:T(8,128)S(1)} %get-tuple-element.25, bf16[2048,3,8,48]{0,3,2,1:T(8,128)(2,1)} %bitcast.59, f32[8,48]{1,0:T(8,128)S(1)} %rsqrt.18, f32[8,48]{1,0:T(8,128)S(1)} %rsqrt.17, f32[8]{0:T(128)S(1)} %copy-done.10, bf16[8,48,48]{2,1,0:T(8,128)(2,1)S(1)} %get-tuple-element.20, ...), kind=kOutput, calls=%fused_computation.43 | convolution fusion | flops 78846384 | bytes 5329408 | tf_op jit(solution)/shard_map/hij,nhj->nhi/dot_general | solution.py:72
  71.4 4.3 %fusion.25 = bf16[2048,1,8,48]{0,3,2,1:T(8,128)(2,1)} fusion(bf16[2048,8,48]{0,2,1:T(8,128)(2,1)} %bitcast.55, f32[8,48]{1,0:T(8,128)S(1)} %get-tuple-element.21, f32[8,48,48]{2,1,0:T(8,128)S(1)} %copy-done.8, f32[8,48]{1,0:T(8,128)S(1)} %rsqrt.18, f32[8,48]{1,0:T(8,128)S(1)} %rsqrt.17, f32[8]{0:T(128)S(1)} %copy-done.10), kind=kOutput, calls=%fused_computation.41 | convolution fusion | flops 76394928 | bytes 3224096 | tf_op jit(solution)/shard_map/nhi,hij->nhj/dot_general | solution.py:74
  75.7 2.6 %pad_maximum_fusion = bf16[2048,3,8,48]{0,3,2,1:T(8,128)(2,1)S(1)} fusion(bf16[2048,1,8,48]{0,3,2,1:T(8,128)(2,1)} %fusion.25, bf16[2048,1,8,48]{0,3,2,1:T(8,128)(2,1)} %fusion.26, bf16[2048,1,8,48]{0,3,2,1:T(8,128)(2,1)} %fusion.27), kind=kLoop, calls=%fused_computation.9 | loop fusion | flops 4718592 | bytes 9437184 | tf_op jit(solution)/shard_map/stack | solution.py:75
  78.3 2.1 %copy-done.6 = bf16[2048,3,8,48]{0,3,2,1:T(8,128)(2,1)} copy-done((bf16[2048,3,8,48]{0,3,2,1:T(8,128)(2,1)}, bf16[2048,3,8,48]{0,3,2,1:T(8,128)(2,1)S(1)}, u32[]{:S(2)}) %copy-start.6) | copy-done | bytes 4718616
  80.5 4.2 %fusion.45 = f32[384,1152]{1,0:T(8,128)} fusion(bf16[2048,1152]{0,1:T(8,128)(2,1)S(1)} %bitcast.62, bf16[2048,384]{1,0:T(8,128)(2,1)S(1)} %copy-done.1, f32[384]{0:T(512)S(1)} %copy-done.12, f32[384]{0:T(512)S(1)} %copy-done.11, f32[2048]{0:T(1024)S(1)} %add_rsqrt_fusion, f32[2048]{0:T(1024)S(1)} %broadcast_multiply_fusion.2), kind=kOutput, calls=%fused_computation.75 | convolution fusion | flops 1816657920 | bytes 8080384 | tf_op jit(solution)/shard_map/nd,nc->dc/dot_general | solution.py:77
  84.6 7.9 %fusion.24 = (f32[384]{0:T(512)S(1)}, f32[2048]{0:T(1024)S(1)}, f32[2048]{0:T(1024)S(1)}, f32[384]{0:T(512)S(1)}, bf16[2048,384]{1,0:T(8,128)(2,1)}) fusion(bf16[2048,384]{1,0:T(8,128)(2,1)S(1)} %copy-done.1, f32[2048]{0:T(1024)S(1)} %add_rsqrt_fusion, f32[2048]{0:T(1024)S(1)} %broadcast_multiply_fusion.2, f32[384]{0:T(512)S(1)} %copy-done.11, ...), kind=kOutput, calls=%fused_computation.36 | convolution fusion | flops 1821371648 | bytes 8786432 | tf_op jit(solution)/shard_map/nc,dc->nd/dot_general | solution.py:76
  92.6 6.3 %all-reduce = (f32[384]{0:T(512)}, f32[384]{0:T(512)}) all-reduce(f32[384]{0:T(512)S(1)} %get-tuple-element.9, f32[384]{0:T(512)S(1)} %get-tuple-element.12), channel_id=1, replica_groups=mesh['dp'=2,'sp'=4] {'sp'}, use_global_device_ids=true, to_apply=%region_18.0 | all-reduce | flops 768 | bytes 6144 | tf_op jit(solution)/shard_map/psum | solution.py:82
  98.9 3.9 %fusion.23 = bf16[2048,384]{1,0:T(8,128)(2,1)} fusion(bf16[2048,384]{1,0:T(8,128)(2,1)S(1)} %copy-done.1, bf16[2048,384]{0,1:T(8,128)(2,1)} %bitcast.65, bf16[384,384]{1,0:T(8,128)(2,1)S(1)} %copy-done.9), kind=kOutput, calls=%fused_computation.35 | convolution fusion | flops 606339072 | bytes 5013504 | tf_op jit(solution)/shard_map/dot_general | solution.py:64
  102.8 2.6 %fusion.14 = bf16[2048,384]{1,0:T(8,128)(2,1)} fusion(bf16[2048,384]{1,0:T(8,128)(2,1)S(1)} %copy-done.1, bf16[2048,384]{1,0:T(8,128)(2,1)S(1)} %copy-done.7, bf16[2048,384]{1,0:T(8,128)(2,1)S(1)} %copy-done.2, f32[2048]{0:T(1024)S(1)} %broadcast_multiply_fusion, f32[2048]{0:T(1024)S(1)} %broadcast_multiply_fusion.1, f32[384]{0:T(512)S(1)} %copy-done.11, ...), kind=kLoop, calls=%fused_computation.26 | loop fusion | flops 9437184 | bytes 6325760 | tf_op jit(solution)/shard_map/convert_element_type | solution.py:79
  105.5 1.6 %convert_element_type.84 = bf16[96,384]{1,0:T(8,128)(2,1)} convert(f32[96,384]{1,0:T(8,128)} %reduce-scatter.5.cloned.1.call-done) | non-fusion elementwise | flops 36864 | bytes 221184 | tf_op jit(solution)/shard_map/convert_element_type | solution.py:81
  107.0 1.4 %reduce-scatter.3.cloned.1.call-done = f32[96,1152]{1,0:T(8,128)} async-done(((f32[384,1152]{1,0:T(8,128)}), f32[96,1152]{1,0:T(8,128)}) %reduce-scatter.3.cloned.1.call-update) | async-done | bytes 442384 | tf_op jit(solution)/shard_map/reduce_scatter | solution.py:80
  108.4 1.7 %convert_element_type.83 = bf16[96,1152]{1,0:T(8,128)(2,1)} convert(f32[96,1152]{1,0:T(8,128)} %reduce-scatter.3.cloned.1.call-done) | non-fusion elementwise | flops 110592 | bytes 663552 | tf_op jit(solution)/shard_map/convert_element_type | solution.py:80
  (33 shorter events, 0.1 us)
Async XLA Ops:
  7.2 4.2 %copy-start = (bf16[384,1152]{1,0:T(8,128)(2,1)S(1)}, bf16[384,1152]{1,0:T(8,128)(2,1)}, u32[]{:S(2)}) copy-start(bf16[384,1152]{1,0:T(8,128)(2,1)} %param.11) | copy-start | bytes 2654212
  7.2 4.2 %copy-start.1 = (bf16[2048,384]{1,0:T(8,128)(2,1)S(1)}, bf16[2048,384]{1,0:T(8,128)(2,1)}, u32[]{:S(2)}) copy-start(bf16[2048,384]{1,0:T(8,128)(2,1)} %param.7) | copy-start | bytes 4718596
  7.2 4.2 %copy-start.11 = (f32[384]{0:T(512)S(1)}, f32[384]{0:T(512)}, u32[]{:S(2)}) copy-start(f32[384]{0:T(512)} %param.9) | copy-start | bytes 4612
  7.2 4.2 %copy-start.12 = (f32[384]{0:T(512)S(1)}, f32[384]{0:T(512)}, u32[]{:S(2)}) copy-start(f32[384]{0:T(512)} %param.10) | copy-start | bytes 4612
  7.2 40.5 %all-reduce.4.cloned.1.call-start = ((), (), s32[]{:S(2)}) async-start(), calls=%async_computation.2 | async-start | bytes 393216 | tf_op jit(solution)/shard_map/psum | solution.py:59
  14.8 2.1 %copy-start.4 = (bf16[2048,1152]{0,1:T(8,128)(2,1)}, bf16[2048,1152]{0,1:T(8,128)(2,1)S(1)}, u32[]{:S(2)}) copy-start(bf16[2048,1152]{0,1:T(8,128)(2,1)S(1)} %convolution_convert_fusion) | copy-start | bytes 14155780
  14.8 3.4 %copy-start.9 = (bf16[384,384]{1,0:T(8,128)(2,1)S(1)}, bf16[384,384]{1,0:T(8,128)(2,1)}, u32[]{:S(2)}) copy-start(bf16[384,384]{1,0:T(8,128)(2,1)} %param.12) | copy-start | bytes 884740
  18.2 87.3 %reduce-scatter.5.cloned.1.call-start = ((), (), s32[]{:S(2)}) async-start(), calls=%async_computation.4 | async-start | bytes 737280 | tf_op jit(solution)/shard_map/reduce_scatter | solution.py:81
  18.2 3.7 %copy-start.5 = (bf16[2048,1152]{0,1:T(8,128)(2,1)S(1)}, bf16[2048,1152]{0,1:T(8,128)(2,1)}, u32[]{:S(2)}) copy-start(bf16[2048,1152]{0,1:T(8,128)(2,1)} %copy-done.4) | copy-start | bytes 14155780
  20.8 1.1 copy-start.3
  22.0 25.7 %copy-start.10 = (f32[8]{0:T(128)S(1)}, f32[8]{0:T(128)}, u32[]{:S(2)}) copy-start(f32[8]{0:T(128)} %param.13) | copy-start | bytes 100
  54.2 4.0 %copy-start.8 = (f32[8,48,48]{2,1,0:T(8,128)S(1)}, f32[8,48,48]{2,1,0:T(8,128)}, u32[]{:S(2)}) copy-start(f32[8,48,48]{2,1,0:T(8,128)} %all-reduce.4.cloned.1.call-done) | copy-start | bytes 221188
  58.0 50.4 %reduce-scatter.3.cloned.1.call-start = ((), (), s32[]{:S(2)}) async-start(), calls=%async_computation.3 | async-start | bytes 2211840 | tf_op jit(solution)/shard_map/reduce_scatter | solution.py:80
  78.3 2.1 %copy-start.6 = (bf16[2048,3,8,48]{0,3,2,1:T(8,128)(2,1)}, bf16[2048,3,8,48]{0,3,2,1:T(8,128)(2,1)S(1)}, u32[]{:S(2)}) copy-start(bf16[2048,3,8,48]{0,3,2,1:T(8,128)(2,1)S(1)} %pad_maximum_fusion) | copy-start | bytes 14155780
  98.9 3.9 %copy-start.2 = (bf16[2048,384]{1,0:T(8,128)(2,1)S(1)}, bf16[2048,384]{1,0:T(8,128)(2,1)}, u32[]{:S(2)}) copy-start(bf16[2048,384]{1,0:T(8,128)(2,1)} %param.8) | copy-start | bytes 4718596
  98.9 3.9 %copy-start.7 = (bf16[2048,384]{1,0:T(8,128)(2,1)S(1)}, bf16[2048,384]{1,0:T(8,128)(2,1)}, u32[]{:S(2)}) copy-start(bf16[2048,384]{1,0:T(8,128)(2,1)} %get-tuple-element.23) | copy-start | bytes 4718596
Sparse Core Ops, SparseCore 0:
  18.3 29.3 all-reduce.3
  58.1 16.4 reduce-scatter.4
  84.8 23.5 reduce-scatter.2
where the time goes:
time: 117 us
  matrix products  46.6 us (40%)
  blocking collectives  22.8 us (19%)
  other arithmetic  18.3 us (16%)
  between operations  14 us (12%)
  waiting for transfers between devices  9.27 us (8%)
  local copies, waits for them, and re-layouts  5.42 us (5%)
    psum x1, blocking collectives, xca_local(): gram, q_sq, k_sq = lax.psum((gram_part, q_sq_part, k_sq_part), 'sp')  16.4 us
    dot_general x1, matrix products, xca_local(): jnp.einsum('nc,dc->nd', d_qkv, w_qkv, preferred_element_type=jnp.float32)  7.91 us
    psum x1, waiting for transfers between devices, xca_local(): gram, q_sq, k_sq = lax.psum((gram_part, q_sq_part, k_sq_part), 'sp')  7.87 us
    psum x1, blocking collectives, xca_local(): d_gamma, d_beta = lax.psum((d_gamma_part, d_beta_part), 'sp')  6.35 us
    dot_general x1, matrix products, xca_local(): jnp.einsum('hij,nhi->nhj', d_gram, query_h, preferred_element_type=jnp.fl...  5.43 us
    unnamed x26, local copies, waits for them, and re-layouts  5.41 us
    dot_general x1, matrix products, xca_local(): jnp.einsum('hij,nhj->nhi', d_gram, key_h, preferred_element_type=jnp.floa...  5.1 us
    dot_general x1, matrix products, xca_local(): jnp.einsum('nhi,hij->nhj', d_out_h, attn, preferred_element_type=jnp.floa...  4.32 us
  transfers between devices with their start and end apart: 3, of which 2 were waited for; matrix products, arithmetic and copies ran while one was open for 38% of the time, Pallas kernels for 0%

commit v1 on v0

v1 whole, which is shorter than its diff:
```python
import jax
import jax.numpy as jnp
from jax import lax
from jax.experimental import pallas as pl
from jax.experimental.pallas import tpu as pltpu
from jax.sharding import PartitionSpec as P

LN_EPS = 1e-6
F32, BF16 = jnp.float32, jnp.bfloat16
MESH = pl.DeviceIdType.MESH

C = 384
HEADS, HD = 8, 48
LANES = 128
TOK = 2048
RB = 512
NB = TOK // RB
SB = 64
OWN = C // 4
PK = 192
W0_HEADS = 5

NN = (((1,), (0,)), ((), ()))
NT = (((1,), (1,)), ((), ()))
TN = (((0,), (0,)), ((), ()))


def mm(a, b, dims=NN):
    return lax.dot_general(a, b, dims, preferred_element_type=F32)


def head_rel():
    lane = lax.broadcasted_iota(jnp.int32, (HD, LANES), 1)
    return [(lane - HD * h) & (LANES - 1) for h in range(HEADS)]


def seg_mask(rel, h, m):
    chan = rel + HD * h
    return (rel < HD) & (chan >= LANES * m) & (chan < LANES * (m + 1))


def head_window(h):
    if h < W0_HEADS:
        return 0, HD * h, (0, 1)
    return 1, HD * h - LANES, (1, 2)


def segs_of(h):
    return sorted({(HD * h) // LANES, (HD * h + HD - 1) // LANES})


def fold_windows(win_refs, out_ref):
    rels = head_rel()
    for p in range(HEADS // 2):
        acc = jnp.zeros((HD, LANES), F32)
        for h in (2 * p, 2 * p + 1):
            w, row, segs = head_window(h)
            for s, m in enumerate(segs):
                if m in segs_of(h):
                    block = win_refs[w][pl.ds(row, HD), pl.ds(LANES * s, LANES)]
                    acc = jnp.where(seg_mask(rels[h], h, m), block, acc)
        out_ref[pl.ds(HD * p, HD), :] = acc


def spread_head(value, rels, h, win_refs):
    w, row, segs = head_window(h)
    parts = []
    for m in segs:
        if m in segs_of(h):
            parts.append(jnp.where(seg_mask(rels[h], h, m), value, 0.0))
        else:
            parts.append(jnp.zeros((HD, LANES), F32))
    win_refs[w][pl.ds(row, HD), :] = jnp.concatenate(parts, axis=1).astype(BF16)


def window_mm(a, win_refs, dims):
    r0 = mm(a[:, :256], win_refs[0][...], dims)
    r1 = mm(a[:, 128:], win_refs[1][...], dims)
    return jnp.concatenate([r0[:, :128], r0[:, 128:] + r1[:, :128], r1[:, 128:]], axis=1)


def kernel(
    x_hbm, dy_hbm, g_hbm, b_hbm, wqkv_hbm, wo_hbm, tau_hbm,
    y, dx, dwqkv_ref, dwo_ref, dg_ref, db_ref, dt_ref,
    x, dy, g_ref, b_ref, wqkv, wo, tau_ref, u, ut, xhat, istd, q, k, v, do, o, ot, dqkv, du,
    g0, g1, sq, pg, rg1, sg, rg2, pa, ra1, sa, ra2,
    a0, a1, e0, e1, attn, score, qk_inv, gfull, dsq,
    wo_part, wv_part, wqk_part, wo_r1, wv_r1, wqk_r1, wo_s, wv_s, wqk_s, wo_r2, wv_r2, wqk_r2,
    dgb_all,
    in_sem, send_sem, recv_sem,
):
    me = lax.axis_index("sp")
    core = lax.rem(me, 2)
    chip = me // 2
    sib = me + 1 - 2 * core
    nbr = lax.rem(me + 2, 4)
    diag = lax.rem(sib + 2, 4)

    n_loads = [0]

    def load(src, dst):
        cp = pltpu.make_async_copy(src, dst, in_sem.at[n_loads[0]])
        n_loads[0] += 1
        cp.start()
        return cp

    def block(i):
        return pl.ds(i * RB, RB)

    ld_gb = [load(g_hbm, g_ref), load(b_hbm, b_ref)]
    ld_x = [load(x_hbm.at[block(0), :], x.at[block(0), :])]
    ld_wqk = load(wqkv_hbm.at[:, pl.ds(0, 2 * C)], wqkv.at[:, pl.ds(0, 2 * C)])
    ld_x += [load(x_hbm.at[block(i), :], x.at[block(i), :]) for i in range(1, NB)]
    ld_wv = load(wqkv_hbm.at[:, pl.ds(2 * C, C)], wqkv.at[:, pl.ds(2 * C, C)])
    ld_wo = load(wo_hbm, wo)
    ld_dy = load(dy_hbm, dy)
    ld_tau = load(tau_hbm, tau_ref)

    barrier = pltpu.get_barrier_semaphore()
    for peer in (sib, nbr, diag):
        pl.semaphore_signal(barrier, inc=1, device_id={"sp": peer}, device_id_type=MESH)

    n_sends = [0]

    def send(src, dst, peer):
        i = n_sends[0]
        n_sends[0] += 1
        cp = pltpu.make_async_remote_copy(
            src_ref=src, dst_ref=dst, send_sem=send_sem.at[i], recv_sem=recv_sem.at[i],
            device_id={"sp": peer}, device_id_type=MESH)
        cp.start()
        return cp

    def step_a(i):
        ld_x[i].wait()
        if i == 0:
            for cp in ld_gb:
                cp.wait()
        gamma = g_ref[...].reshape(1, C)
        beta = b_ref[...].reshape(1, C)
        for j in range(RB // SB):
            rows = pl.ds(i * RB + j * SB, SB)
            xf = x[rows, :].astype(F32)
            cen = xf - jnp.mean(xf, axis=-1, keepdims=True)
            inv = lax.rsqrt(jnp.mean(cen * cen, axis=-1, keepdims=True) + LN_EPS)
            xh = cen * inv
            xhat[rows, :] = xh
            istd[rows, :] = jnp.broadcast_to(inv, (SB, LANES))
            u[rows, :] = (xh * gamma + beta).astype(BF16)
        rows = block(i)
        if i == 0:
            ld_wqk.wait()
        q[rows, :] = mm(u[rows, :], wqkv[:, :C]).astype(BF16)
        k[rows, :] = mm(u[rows, :], wqkv[:, C : 2 * C]).astype(BF16)
        p0 = mm(q[rows, :256], k[rows, :256], TN)
        p1 = mm(q[rows, 128:], k[rows, 128:], TN)
        part = jnp.zeros((8, 2 * C), F32)
        for j in range(RB // SB):
            sub = pl.ds(i * RB + j * SB, SB)
            qkf = jnp.concatenate([q[sub, :], k[sub, :]], axis=1).astype(F32)
            part += jnp.sum((qkf * qkf).reshape(SB // 8, 8, 2 * C), axis=0)
        if i == 0:
            g0[...], g1[...], sq[...] = p0, p1, part
        else:
            g0[...] += p0
            g1[...] += p1
            sq[...] += part
        ut[:, rows] = u[rows, :].T

    with jax.named_scope("ln_qk"):
        for i in range(NB):
            step_a(i)
    with jax.named_scope("fold_g"):
        fold_windows((g0, g1), pg)
        sums = jnp.sum(sq[...], axis=0, keepdims=True)
        for m in range(6):
            pg[pl.ds(PK + m, 1), :] = sums[:, LANES * m : LANES * (m + 1)]
        pg[pl.ds(PK + 6, 2), :] = jnp.zeros((2, LANES), F32)
    with jax.named_scope("greet"):
        pl.semaphore_wait(barrier, 3)
    s_g1 = send(pg, rg1, sib)

    def step_b(i):
        rows = block(i)
        v[rows, :] = mm(u[rows, :], wqkv[:, 2 * C :]).astype(BF16)
        do[rows, :] = mm(dy[rows, :], wo[...], NT).astype(BF16)
        p0 = mm(do[rows, :256], v[rows, :256], TN)
        p1 = mm(do[rows, 128:], v[rows, 128:], TN)
        if i == 0:
            g0[...], g1[...] = p0, p1
        else:
            g0[...] += p0
            g1[...] += p1

    with jax.named_scope("v_do_1"):
        ld_wv.wait()
        ld_wo.wait()
        ld_dy.wait()
        ld_tau.wait()
        for i in range(NB // 2):
            step_b(i)
    with jax.named_scope("sum_g"):
        s_g1.wait()
        sg[...] = pg[...] + rg1[...]
        s_g2 = send(sg, rg2, nbr)
    with jax.named_scope("v_do_2"):
        for i in range(NB // 2, NB):
            step_b(i)
    with jax.named_scope("fold_a"):
        fold_windows((g0, g1), pa)
        s_a1 = send(pa, ra1, sib)
    with jax.named_scope("sum_a"):
        s_a1.wait()
        sa[...] = pa[...] + ra1[...]
        s_a2 = send(sa, ra2, nbr)

    with jax.named_scope("wait_g"):
        s_g2.wait()
    rels = head_rel()
    row = lax.broadcasted_iota(jnp.int32, (HD, LANES), 0)
    with jax.named_scope("softmax"):
        gfull[...] = sg[...] + rg2[...]
        for ref in (a0, a1, e0, e1):
            ref[...] = jnp.zeros_like(ref)
        for h in range(HEADS):
            rel = rels[h]
            valid = rel < HD
            tau = tau_ref[h]
            s_q = jnp.zeros((HD, LANES), F32)
            s_k = jnp.ones((HD, LANES), F32)
            for m in segs_of(h):
                mask = seg_mask(rel, h, m)
                s_q = jnp.where(mask, gfull[pl.ds(PK + m, 1), :], s_q)
                s_k = jnp.where(mask, gfull[pl.ds(PK + 3 + m, 1), :], s_k)
            s_q = jnp.sum(jnp.where(rel == row, s_q, 0.0), axis=1, keepdims=True)
            inv = jnp.where(valid, lax.rsqrt(s_q) * lax.rsqrt(s_k), 0.0)
            gram = jnp.where(valid, gfull[pl.ds(HD * (h // 2), HD), :], 0.0)
            sc = tau * gram * inv
            top = jnp.max(jnp.where(valid, sc, -jnp.inf), axis=1, keepdims=True)
            ex = jnp.where(valid, jnp.exp(sc - top), 0.0)
            at = ex / jnp.sum(ex, axis=1, keepdims=True)
            hr = pl.ds(HD * h, HD)
            score[hr, :] = sc
            qk_inv[hr, :] = inv
            attn[hr, :] = at
            spread_head(at, rels, h, (a0, a1))

    far = pl.ds(pl.multiple_of(2 * OWN * (1 - chip), 16), 2 * OWN)
    near = pl.ds(pl.multiple_of(2 * OWN * chip, 16), 2 * OWN)
    theirs = pl.ds(pl.multiple_of(OWN * (1 - core), 8), OWN)
    mine = pl.ds(pl.multiple_of(OWN * core, 8), OWN)

    def part_rows(lhs_t, rows, rhs, part, r1, slot):
        part[slot] = mm(lhs_t[rows, :], rhs)
        return send(part.at[slot, theirs, :], r1.at[slot], sib)

    def cross(cp, part, r1, s, r2):
        cp.wait()
        s[...] = part[0, mine, :] + r1[0]
        return send(s, r2, nbr)

    with jax.named_scope("o"):
        for i in range(NB):
            rows = block(i)
            o[rows, :] = window_mm(v[rows, :], (a0, a1), NT).astype(BF16)
            ot[:, rows] = o[rows, :].T
    with jax.named_scope("dwo_far"):
        f_wo = part_rows(ot, far, dy[...], wo_part, wo_r1, 0)
    with jax.named_scope("dv"):
        for i in range(NB):
            rows = block(i)
            dqkv[rows, 2 * C :] = window_mm(do[rows, :], (a0, a1), NN).astype(BF16)
    with jax.named_scope("cross_wo"):
        x_wo = cross(f_wo, wo_part, wo_r1, wo_s, wo_r2)
    with jax.named_scope("dwv_far"):
        f_wv = part_rows(ut, far, dqkv[:, 2 * C :], wv_part, wv_r1, 0)

    with jax.named_scope("wait_a"):
        s_a2.wait()
    with jax.named_scope("softmax_bwd"):
        dsum = [jnp.zeros((1, LANES), F32) for _ in range(6)]
        lane = lax.broadcasted_iota(jnp.int32, (1, LANES), 1)
        d_tau = jnp.zeros((1, LANES), F32)
        for h in range(HEADS):
            rel = rels[h]
            valid = rel < HD
            hr = pl.ds(HD * h, HD)
            pr = pl.ds(HD * (h // 2), HD)
            at = attn[hr, :]
            d_at = jnp.where(valid, sa[pr, :] + ra2[pr, :], 0.0).astype(BF16).astype(F32)
            d_sc = at * (d_at - jnp.sum(d_at * at, axis=1, keepdims=True))
            d_sc_inv = d_sc * qk_inv[hr, :]
            d_tau_h = jnp.sum(d_sc_inv * jnp.where(valid, gfull[pr, :], 0.0), axis=0, keepdims=True)
            d_tau = jnp.where(lane == h, jnp.sum(d_tau_h, axis=1, keepdims=True), d_tau)
            spread_head(d_sc_inv * tau_ref[h], rels, h, (e0, e1))
            wt = d_sc * score[hr, :]
            over_q = jnp.sum(jnp.where(rel == row, jnp.sum(wt, axis=1, keepdims=True), 0.0), axis=0, keepdims=True)
            over_k = jnp.sum(wt, axis=0, keepdims=True)
            for m in segs_of(h):
                mask = seg_mask(rel, h, m)[:1]
                dsum[m] = jnp.where(mask, over_q, dsum[m])
                dsum[3 + m] = jnp.where(mask, over_k, dsum[3 + m])
        dt_ref[...] = d_tau[:, :HEADS].reshape(HEADS)
        for m in range(6):
            dsq[:, pl.ds(LANES * m, LANES)] = -dsum[m] / gfull[pl.ds(PK + m, 1), :]
    with jax.named_scope("cross_wv"):
        x_wv = cross(f_wv, wv_part, wv_r1, wv_s, wv_r2)

    with jax.named_scope("dqk"):
        for i in range(NB):
            rows = block(i)
            dqkv[rows, :C] = (
                window_mm(k[rows, :], (e0, e1), NT) + q[rows, :].astype(F32) * dsq[:, :C]).astype(BF16)
            dqkv[rows, C : 2 * C] = (
                window_mm(q[rows, :], (e0, e1), NN) + k[rows, :].astype(F32) * dsq[:, C:]).astype(BF16)
    with jax.named_scope("dwqk_far"):
        f_wqk = part_rows(ut, far, dqkv[:, : 2 * C], wqk_part, wqk_r1, 0)
    with jax.named_scope("near"):
        l_wo = part_rows(ot, near, dy[...], wo_part, wo_r1, 1)
        l_wv = part_rows(ut, near, dqkv[:, 2 * C :], wv_part, wv_r1, 1)
    with jax.named_scope("cross_wqk"):
        x_wqk = cross(f_wqk, wqk_part, wqk_r1, wqk_s, wqk_r2)
    with jax.named_scope("near_qk"):
        l_wqk = part_rows(ut, near, dqkv[:, : 2 * C], wqk_part, wqk_r1, 1)

    gamma = g_ref[...].reshape(1, C)
    dgam = jnp.zeros((8, C), F32)
    dbet = jnp.zeros((8, C), F32)
    with jax.named_scope("ln_bwd"):
        for i in range(NB):
            rows = block(i)
            du[rows, :] = mm(dqkv[rows, :], wqkv[...], NT).astype(BF16)
            for j in range(RB // SB):
                sub = pl.ds(i * RB + j * SB, SB)
                d = du[sub, :].astype(F32)
                xh = xhat[sub, :]
                dxh = d * xh
                dgam += jnp.sum(dxh.reshape(SB // 8, 8, C), axis=0)
                dbet += jnp.sum(d.reshape(SB // 8, 8, C), axis=0)
                dh = d * gamma
                m1 = jnp.mean(dh, axis=-1, keepdims=True)
                m2 = jnp.mean(dxh * gamma, axis=-1, keepdims=True)
                inv = istd[sub, :]
                term = dh - m1 - xh * m2
                dln = term * jnp.concatenate([inv, inv, inv], axis=1)
                dx[sub, :] = (dy[sub, :].astype(F32) + dln).astype(BF16)
        dgb_all[me] = jnp.concatenate(
            [jnp.sum(dgam, axis=0, keepdims=True), jnp.sum(dbet, axis=0, keepdims=True), jnp.zeros((6, C), F32)],
            axis=0)
    c_dgb = [send(dgb_all.at[me], dgb_all.at[me], peer) for peer in (sib, nbr, diag)]
    with jax.named_scope("y"):
        for i in range(NB):
            rows = block(i)
            y[rows, :] = (x[rows, :].astype(F32) + mm(o[rows, :], wo[...])).astype(BF16)

    with jax.named_scope("wait_wo"):
        l_wo.wait()
        x_wo.wait()
        dwo_ref[...] = (wo_part[1, mine, :] + wo_r1[1] + wo_r2[...]).astype(BF16)
    with jax.named_scope("wait_wv"):
        l_wv.wait()
        x_wv.wait()
        dwqkv_ref[:, 2 * C :] = (wv_part[1, mine, :] + wv_r1[1] + wv_r2[...]).astype(BF16)
    with jax.named_scope("wait_dgb"):
        for cp in c_dgb:
            cp.wait()
        total = dgb_all[0] + dgb_all[1] + dgb_all[2] + dgb_all[3]
        dg_ref[...] = total[0:1].reshape(C)
        db_ref[...] = total[1:2].reshape(C)
    with jax.named_scope("wait_wqk"):
        l_wqk.wait()
        x_wqk.wait()
        dwqkv_ref[:, : 2 * C] = (wqk_part[1, mine, :] + wqk_r1[1] + wqk_r2[...]).astype(BF16)


def write_out(*refs):
    ins, outs, sem = refs[:7], refs[7:14], refs[14]
    copies = [pltpu.make_async_copy(ins[i], outs[i], sem.at[i]) for i in range(7)]
    for cp in copies:
        cp.start()
    for cp in copies:
        cp.wait()


def xca_local(x_rows, dy_rows, ln_gamma, ln_beta, w_qkv, w_out, temperature):
    vm = pltpu.VMEM
    hbm_spec = pl.BlockSpec(memory_space=pltpu.HBM)
    vmem_spec = pl.BlockSpec(memory_space=pltpu.VMEM)
    results = (
        ((TOK, C), BF16), ((TOK, C), BF16), ((OWN, 3 * C), BF16), ((OWN, C), BF16),
        ((C,), F32), ((C,), F32), ((HEADS,), F32),
    )
    rows_bf = vm((TOK, C), BF16)
    cols_bf = vm((C, TOK), BF16)
    win_f = vm((256, 256), F32)
    win_b = vm((256, 256), BF16)
    pk_g = vm((PK + 8, LANES), F32)
    pk_a = vm((PK, LANES), F32)
    fold = vm((C, LANES), F32)
    scratch = [
        rows_bf, rows_bf, vm((C,), F32), vm((C,), F32), vm((C, 3 * C), BF16), vm((C, C), BF16),
        pltpu.SMEM((HEADS,), F32), rows_bf, cols_bf, vm((TOK, C), F32), vm((TOK, LANES), F32),
        rows_bf, rows_bf, rows_bf, rows_bf, rows_bf, cols_bf, vm((TOK, 3 * C), BF16), rows_bf,
        win_f, win_f, vm((8, 2 * C), F32), pk_g, pk_g, pk_g, pk_g, pk_a, pk_a, pk_a, pk_a,
        win_b, win_b, win_b, win_b, fold, fold, fold, pk_g, vm((1, 2 * C), F32),
        vm((2, 2 * OWN, C), F32), vm((2, 2 * OWN, C), F32), vm((2, 2 * OWN, 2 * C), F32),
        vm((2, OWN, C), F32), vm((2, OWN, C), F32), vm((2, OWN, 2 * C), F32),
        vm((OWN, C), F32), vm((OWN, C), F32), vm((OWN, 2 * C), F32),
        vm((OWN, C), F32), vm((OWN, C), F32), vm((OWN, 2 * C), F32),
        vm((4, 8, C), F32),
        pltpu.SemaphoreType.DMA((12,)),
        pltpu.SemaphoreType.DMA((16,)), pltpu.SemaphoreType.DMA((16,)),
    ]
    parts = pl.pallas_call(
        kernel,
        name="xca",
        out_shape=tuple(pltpu.VMEM(shape, dtype) for shape, dtype in results),
        in_specs=[hbm_spec] * 7,
        out_specs=[vmem_spec] * 7,
        scratch_shapes=scratch,
        compiler_params=pltpu.CompilerParams(
            collective_id=0, has_side_effects=True, vmem_limit_bytes=60 * 1024 * 1024),
    )(x_rows, dy_rows, ln_gamma, ln_beta, w_qkv, w_out, temperature)
    return pl.pallas_call(
        write_out,
        name="xca_out",
        out_shape=tuple(jax.ShapeDtypeStruct(shape, dtype) for shape, dtype in results),
        in_specs=[vmem_spec] * 7,
        out_specs=[hbm_spec] * 7,
        scratch_shapes=[pltpu.SemaphoreType.DMA((7,))],
        compiler_params=pltpu.CompilerParams(vmem_limit_bytes=1024 * 1024),
    )(*parts)


def solution(mesh):
    row_spec = P(('dp', 'sp'), None)
    full_mat = P(None, None)
    full_vec = P(None)
    part_vec = P('dp')
    return jax.shard_map(
        xca_local, mesh=mesh,
        in_specs=(row_spec, row_spec, full_vec, full_vec, full_mat, full_mat, full_vec),
        out_specs=(row_spec, row_spec, row_spec, row_spec, part_vec, part_vec, part_vec),
        check_vma=False)
```

time: 117 us -> 33.8 us (0.29)
  matrix products: 46.6 us -> 0 us
  Pallas kernels: 0 us -> 32.9 us
  blocking collectives: 22.8 us -> 0 us
  other arithmetic: 18.3 us -> 0 us
  between operations: 14 us -> 0.8 us
  waiting for transfers between devices: 9.27 us -> 0 us
  local copies, waits for them, and re-layouts: 5.42 us -> 0 us
    dot_general x12 -> x0, matrix products: 46.6 us -> none  [the longest x1 7.91 us: xca_local(): jnp.einsum('nc,dc->nd', d_qkv, w_qkv, preferred_element_type=jnp.float32)]
    pallas_call x0 -> x2, Pallas kernels: none -> 32.9 us  [the longest x1 31.1 us: xca_local(): pl.pallas_call(kernel, name='xca', out_shape=tuple((pltpu.VMEM(shape, dty...]
    psum x2 -> x0, blocking collectives: 22.8 us -> none  [the longest x1 16.4 us: xca_local(): gram, q_sq, k_sq = lax.psum((gram_part, q_sq_part, k_sq_part), 'sp')]
    psum x1 -> x0, waiting for transfers between devices: 7.87 us -> none  [xca_local(): gram, q_sq, k_sq = lax.psum((gram_part, q_sq_part, k_sq_part), 'sp')]
    convert_element_type x3 -> x0, other arithmetic: 5.92 us -> none  [the longest x1 2.64 us: xca_local(): dx_rows = (dy_rows.astype(jnp.float32) + d_ln).astype(jnp.bfloat16)]
    unnamed x26 -> x0, local copies, waits for them, and re-layouts: 5.41 us -> none
    sub x2 -> x0, other arithmetic: 4.96 us -> none  [the longest x1 2.63 us: state_softmax_bwd(): d_attn - jnp.sum(d_attn * attn_f32, axis=-1, keepdims=True)]
    reduce_sum x3 -> x0, other arithmetic: 4.79 us -> none  [the longest x1 2.2 us: layer_norm_fwd(): jnp.mean(centered * centered, axis=-1, keepdims=True) + LN_EPS]
  transfers between devices with their start and end apart: 3 -> 0, of which waited for: 2 -> 0; matrix products, arithmetic and copies ran while one was open for 38% -> 0% of each run, Pallas kernels for 0% -> 0%
where the time goes in v1:
time: 33.8 us; the launch traced here: 33.7 us
  Pallas kernels  32.9 us (97%)
  between operations  0.8 us (2%)
    pallas_call x1, Pallas kernels, xca_local(): pl.pallas_call(kernel, name='xca', out_shape=tuple((pltpu.VMEM(shape, dty...  31.1 us
    pallas_call x1, Pallas kernels, xca_local(): pl.pallas_call(write_out, name='xca_out', out_shape=tuple((jax.ShapeDtype...  1.81 us

profile of v1, /device:TPU:0, one launch (start us, length us, event | category | flops | bytes accessed | tf_op | source)
XLA Modules:
  0.0 33.7 jit_solution(16673980491370815952)
XLA Ops:
  0.6 31.1 %xca.1 = (bf16[2048,384]{1,0:T(8,128)(2,1)S(1)}, bf16[2048,384]{1,0:T(8,128)(2,1)S(1)}, bf16[96,1152]{1,0:T(8,128)(2,1)S(1)}, bf16[96,384]{1,0:T(8,128)(2,1)S(1)...) custom-call(bf16[2048,384]{1,0:T(8,128)(2,1)} %x_hbm.1, bf16[2048,384]{1,0:T(8,128)(2,1)} %dy_hbm.1, f32[384]{0:T(512)} %g_hbm.1, ...), custom_call_target="tpu_custom_call" | custom-call | tf_op jit(solution)/shard_map/xca/pallas_call | solution.py:414
  31.7 1.8 %xca_out.1 = (bf16[2048,384]{1,0:T(8,128)(2,1)}, bf16[2048,384]{1,0:T(8,128)(2,1)}, bf16[96,1152]{1,0:T(8,128)(2,1)}, bf16[96,384]{1,0:T(8,128)(2,1)}, f32[384]{0:T(512)}, /*index=5*/f32[384]{0:T(512)}, f32[8]{0:T(128)}) custom-call(bf16[2048,384]{1,0:T(8,128)(2,1)S(1)} %get-tuple-element.14.refs_0_, bf16[2048,384]{1,0:T(8,128)(2,1)S(1)} %get-tuple-element.15.refs_1_, ...), custom_call_target="tpu_custom_call" | custom-call | tf_op jit(solution)/shard_map/xca_out/pallas_call | solution.py:424

commit v2 on v1

--- a/solution.py
+++ b/solution.py
@@ -15,9 +15,15 @@
 TOK = 2048
 RB = 512
 NB = TOK // RB
+RA = 512
+NA = TOK // RA
+RV = 256
+NV = TOK // RV
+CUT = 3
+PIECES = 4
 SB = 64
 OWN = C // 4
-PK = 192
+PK = 144
 W0_HEADS = 5
 
 NN = (((1,), (0,)), ((), ()))
@@ -49,17 +55,34 @@
     return sorted({(HD * h) // LANES, (HD * h + HD - 1) // LANES})
 
 
+def spare_lanes(g):
+    lane = lax.broadcasted_iota(jnp.int32, (HD, LANES), 1)
+    return (lane >= 96 - 32 * g) & (lane < 128 - 32 * g)
+
+
 def fold_windows(win_refs, out_ref):
     rels = head_rel()
-    for p in range(HEADS // 2):
-        acc = jnp.zeros((HD, LANES), F32)
-        for h in (2 * p, 2 * p + 1):
-            w, row, segs = head_window(h)
-            for s, m in enumerate(segs):
-                if m in segs_of(h):
-                    block = win_refs[w][pl.ds(row, HD), pl.ds(LANES * s, LANES)]
-                    acc = jnp.where(seg_mask(rels[h], h, m), block, acc)
-        out_ref[pl.ds(HD * p, HD), :] = acc
+
+    def put(acc, h, where):
+        w, row, segs = head_window(h)
+        for s, m in enumerate(segs):
+            if m in segs_of(h):
+                block = win_refs[w][pl.ds(row, HD), pl.ds(LANES * s, LANES)]
+                mask = seg_mask(rels[h], h, m)
+                acc = jnp.where(mask if where is None else mask & where, block, acc)
+        return acc
+
+    for g in range(3):
+        acc = put(put(jnp.zeros((HD, LANES), F32), 2 * g, None), 2 * g + 1, None)
+        spare = spare_lanes(g)
+        out_ref[pl.ds(HD * g, HD), :] = put(put(acc, 6, spare), 7, spare)
+
+
+def packed_head(ref, h):
+    if h < 6:
+        return ref[pl.ds(HD * (h // 2), HD), :]
+    lane = lax.broadcasted_iota(jnp.int32, (HD, LANES), 1)
+    return jnp.where(lane >= 96, ref[pl.ds(0, HD), :], jnp.where(lane >= 64, ref[pl.ds(HD, HD), :], ref[pl.ds(2 * HD, HD), :]))
 
 
 def spread_head(value, rels, h, win_refs):
@@ -82,7 +105,7 @@
 def kernel(
     x_hbm, dy_hbm, g_hbm, b_hbm, wqkv_hbm, wo_hbm, tau_hbm,
     y, dx, dwqkv_ref, dwo_ref, dg_ref, db_ref, dt_ref,
-    x, dy, g_ref, b_ref, wqkv, wo, tau_ref, u, ut, xhat, istd, q, k, v, do, o, ot, dqkv, du,
+    x, dy, g_ref, b_ref, wqkv, wo, wot, tau_ref, u, ut, xhat, istd, q, k, v, do, o, ot, dqkv, du,
     g0, g1, sq, pg, rg1, sg, rg2, pa, ra1, sa, ra2,
     a0, a1, e0, e1, attn, score, qk_inv, gfull, dsq,
     wo_part, wv_part, wqk_part, wo_r1, wv_r1, wqk_r1, wo_s, wv_s, wqk_s, wo_r2, wv_r2, wqk_r2,
@@ -108,11 +131,11 @@
         return pl.ds(i * RB, RB)
 
     ld_gb = [load(g_hbm, g_ref), load(b_hbm, b_ref)]
-    ld_x = [load(x_hbm.at[block(0), :], x.at[block(0), :])]
+    ld_x = [load(x_hbm.at[pl.ds(0, RA), :], x.at[pl.ds(0, RA), :])]
     ld_wqk = load(wqkv_hbm.at[:, pl.ds(0, 2 * C)], wqkv.at[:, pl.ds(0, 2 * C)])
-    ld_x += [load(x_hbm.at[block(i), :], x.at[block(i), :]) for i in range(1, NB)]
+    ld_x += [load(x_hbm.at[pl.ds(i * RA, RA), :], x.at[pl.ds(i * RA, RA), :]) for i in range(1, NA)]
+    ld_wo = load(wo_hbm, wo)
     ld_wv = load(wqkv_hbm.at[:, pl.ds(2 * C, C)], wqkv.at[:, pl.ds(2 * C, C)])
-    ld_wo = load(wo_hbm, wo)
     ld_dy = load(dy_hbm, dy)
     ld_tau = load(tau_hbm, tau_ref)
 
@@ -131,15 +154,11 @@
         cp.start()
         return cp
 
-    def step_a(i):
-        ld_x[i].wait()
-        if i == 0:
-            for cp in ld_gb:
-                cp.wait()
+    def step_ln(i):
         gamma = g_ref[...].reshape(1, C)
         beta = b_ref[...].reshape(1, C)
-        for j in range(RB // SB):
-            rows = pl.ds(i * RB + j * SB, SB)
+        for j in range(RA // SB):
+            rows = pl.ds(i * RA + j * SB, SB)
             xf = x[rows, :].astype(F32)
             cen = xf - jnp.mean(xf, axis=-1, keepdims=True)
             inv = lax.rsqrt(jnp.mean(cen * cen, axis=-1, keepdims=True) + LN_EPS)
@@ -147,29 +166,51 @@
             xhat[rows, :] = xh
             istd[rows, :] = jnp.broadcast_to(inv, (SB, LANES))
             u[rows, :] = (xh * gamma + beta).astype(BF16)
-        rows = block(i)
-        if i == 0:
-            ld_wqk.wait()
-        q[rows, :] = mm(u[rows, :], wqkv[:, :C]).astype(BF16)
-        k[rows, :] = mm(u[rows, :], wqkv[:, C : 2 * C]).astype(BF16)
+
+    def step_qk(i):
+        rows = pl.ds(i * RA, RA)
+        qk = mm(u[rows, :], wqkv[:, : 2 * C]).astype(BF16)
+        q[rows, :] = qk[:, :C]
+        k[rows, :] = qk[:, C:]
+
+    def step_gram(i):
+        rows = pl.ds(i * RA, RA)
         p0 = mm(q[rows, :256], k[rows, :256], TN)
         p1 = mm(q[rows, 128:], k[rows, 128:], TN)
-        part = jnp.zeros((8, 2 * C), F32)
-        for j in range(RB // SB):
-            sub = pl.ds(i * RB + j * SB, SB)
-            qkf = jnp.concatenate([q[sub, :], k[sub, :]], axis=1).astype(F32)
-            part += jnp.sum((qkf * qkf).reshape(SB // 8, 8, 2 * C), axis=0)
         if i == 0:
-            g0[...], g1[...], sq[...] = p0, p1, part
+            g0[...], g1[...] = p0, p1
         else:
             g0[...] += p0
             g1[...] += p1
-            sq[...] += part
+        for r, c0 in ((q, 0), (k, C)):
+            part = jnp.zeros((8, C), F32)
+            for j in range(RA // SB):
+                f = r[pl.ds(i * RA + j * SB, SB), :].astype(F32)
+                part += jnp.sum((f * f).reshape(SB // 8, 8, C), axis=0)
+            if i == 0:
+                sq[:, pl.ds(c0, C)] = part
+            else:
+                sq[:, pl.ds(c0, C)] += part
         ut[:, rows] = u[rows, :].T
 
+    with jax.named_scope("ln_0"):
+        ld_x[0].wait()
+        for cp in ld_gb:
+            cp.wait()
+        step_ln(0)
+    ld_wqk.wait()
+    for cp in ld_x[1:]:
+        cp.wait()
+    ld_wo.wait()
     with jax.named_scope("ln_qk"):
-        for i in range(NB):
-            step_a(i)
+        wot[...] = wo[...].T
+        for i in range(1, NA + 2):
+            if i < NA:
+                step_ln(i)
+            if 1 <= i <= NA:
+                step_qk(i - 1)
+            if i >= 2:
+                step_gram(i - 2)
     with jax.named_scope("fold_g"):
         fold_windows((g0, g1), pg)
         sums = jnp.sum(sq[...], axis=0, keepdims=True)
@@ -181,9 +222,12 @@
     s_g1 = send(pg, rg1, sib)
 
     def step_b(i):
-        rows = block(i)
+        rows = pl.ds(i * RV, RV)
         v[rows, :] = mm(u[rows, :], wqkv[:, 2 * C :]).astype(BF16)
-        do[rows, :] = mm(dy[rows, :], wo[...], NT).astype(BF16)
+        do[rows, :] = mm(dy[rows, :], wot[...]).astype(BF16)
+
+    def step_da(i):
+        rows = pl.ds(i * RV, RV)
         p0 = mm(do[rows, :256], v[rows, :256], TN)
         p1 = mm(do[rows, 128:], v[rows, 128:], TN)
         if i == 0:
@@ -194,18 +238,23 @@
 
     with jax.named_scope("v_do_1"):
         ld_wv.wait()
-        ld_wo.wait()
         ld_dy.wait()
         ld_tau.wait()
-        for i in range(NB // 2):
-            step_b(i)
+        for i in range(CUT + 1):
+            if i < CUT:
+                step_b(i)
+            if i >= 1:
+                step_da(i - 1)
     with jax.named_scope("sum_g"):
         s_g1.wait()
         sg[...] = pg[...] + rg1[...]
         s_g2 = send(sg, rg2, nbr)
     with jax.named_scope("v_do_2"):
-        for i in range(NB // 2, NB):
-            step_b(i)
+        for i in range(CUT, NV + 1):
+            if i < NV:
+                step_b(i)
+            if i >= CUT + 1:
+                step_da(i - 1)
     with jax.named_scope("fold_a"):
         fold_windows((g0, g1), pa)
         s_a1 = send(pa, ra1, sib)
@@ -234,7 +283,7 @@
                 s_k = jnp.where(mask, gfull[pl.ds(PK + 3 + m, 1), :], s_k)
             s_q = jnp.sum(jnp.where(rel == row, s_q, 0.0), axis=1, keepdims=True)
             inv = jnp.where(valid, lax.rsqrt(s_q) * lax.rsqrt(s_k), 0.0)
-            gram = jnp.where(valid, gfull[pl.ds(HD * (h // 2), HD), :], 0.0)
+            gram = jnp.where(valid, packed_head(gfull, h), 0.0)
             sc = tau * gram * inv
             top = jnp.max(jnp.where(valid, sc, -jnp.inf), axis=1, keepdims=True)
             ex = jnp.where(valid, jnp.exp(sc - top), 0.0)
@@ -259,21 +308,20 @@
         s[...] = part[0, mine, :] + r1[0]
         return send(s, r2, nbr)
 
+    with jax.named_scope("dv"):
+        for i in range(NB):
+            rows = block(i)
+            dqkv[rows, 2 * C :] = window_mm(do[rows, :], (a0, a1), NN).astype(BF16)
+        f_wv = part_rows(ut, far, dqkv[:, 2 * C :], wv_part, wv_r1, 0)
     with jax.named_scope("o"):
         for i in range(NB):
             rows = block(i)
             o[rows, :] = window_mm(v[rows, :], (a0, a1), NT).astype(BF16)
             ot[:, rows] = o[rows, :].T
+    with jax.named_scope("cross_wv"):
+        x_wv = cross(f_wv, wv_part, wv_r1, wv_s, wv_r2)
     with jax.named_scope("dwo_far"):
         f_wo = part_rows(ot, far, dy[...], wo_part, wo_r1, 0)
-    with jax.named_scope("dv"):
-        for i in range(NB):
-            rows = block(i)
-            dqkv[rows, 2 * C :] = window_mm(do[rows, :], (a0, a1), NN).astype(BF16)
-    with jax.named_scope("cross_wo"):
-        x_wo = cross(f_wo, wo_part, wo_r1, wo_s, wo_r2)
-    with jax.named_scope("dwv_far"):
-        f_wv = part_rows(ut, far, dqkv[:, 2 * C :], wv_part, wv_r1, 0)
 
     with jax.named_scope("wait_a"):
         s_a2.wait()
@@ -285,12 +333,11 @@
             rel = rels[h]
             valid = rel < HD
             hr = pl.ds(HD * h, HD)
-            pr = pl.ds(HD * (h // 2), HD)
             at = attn[hr, :]
-            d_at = jnp.where(valid, sa[pr, :] + ra2[pr, :], 0.0).astype(BF16).astype(F32)
+            d_at = jnp.where(valid, packed_head(sa, h) + packed_head(ra2, h), 0.0).astype(BF16).astype(F32)
             d_sc = at * (d_at - jnp.sum(d_at * at, axis=1, keepdims=True))
             d_sc_inv = d_sc * qk_inv[hr, :]
-            d_tau_h = jnp.sum(d_sc_inv * jnp.where(valid, gfull[pr, :], 0.0), axis=0, keepdims=True)
+            d_tau_h = jnp.sum(d_sc_inv * jnp.where(valid, packed_head(gfull, h), 0.0), axis=0, keepdims=True)
             d_tau = jnp.where(lane == h, jnp.sum(d_tau_h, axis=1, keepdims=True), d_tau)
             spread_head(d_sc_inv * tau_ref[h], rels, h, (e0, e1))
             wt = d_sc * score[hr, :]
@@ -303,8 +350,8 @@
         dt_ref[...] = d_tau[:, :HEADS].reshape(HEADS)
         for m in range(6):
             dsq[:, pl.ds(LANES * m, LANES)] = -dsum[m] / gfull[pl.ds(PK + m, 1), :]
-    with jax.named_scope("cross_wv"):
-        x_wv = cross(f_wv, wv_part, wv_r1, wv_s, wv_r2)
+    with jax.named_scope("cross_wo"):
+        x_wo = cross(f_wo, wo_part, wo_r1, wo_s, wo_r2)
 
     with jax.named_scope("dqk"):
         for i in range(NB):
@@ -316,11 +363,11 @@
     with jax.named_scope("dwqk_far"):
         f_wqk = part_rows(ut, far, dqkv[:, : 2 * C], wqk_part, wqk_r1, 0)
     with jax.named_scope("near"):
-        l_wo = part_rows(ot, near, dy[...], wo_part, wo_r1, 1)
         l_wv = part_rows(ut, near, dqkv[:, 2 * C :], wv_part, wv_r1, 1)
     with jax.named_scope("cross_wqk"):
         x_wqk = cross(f_wqk, wqk_part, wqk_r1, wqk_s, wqk_r2)
     with jax.named_scope("near_qk"):
+        l_wo = part_rows(ot, near, dy[...], wo_part, wo_r1, 1)
         l_wqk = part_rows(ut, near, dqkv[:, : 2 * C], wqk_part, wqk_r1, 1)
 
     gamma = g_ref[...].reshape(1, C)
@@ -345,8 +392,7 @@
                 dln = term * jnp.concatenate([inv, inv, inv], axis=1)
                 dx[sub, :] = (dy[sub, :].astype(F32) + dln).astype(BF16)
         dgb_all[me] = jnp.concatenate(
-            [jnp.sum(dgam, axis=0, keepdims=True), jnp.sum(dbet, axis=0, keepdims=True), jnp.zeros((6, C), F32)],
-            axis=0)
+            [jnp.sum(dgam, axis=0, keepdims=True), jnp.sum(dbet, axis=0, keepdims=True)], axis=1)
     c_dgb = [send(dgb_all.at[me], dgb_all.at[me], peer) for peer in (sib, nbr, diag)]
     with jax.named_scope("y"):
         for i in range(NB):
@@ -365,8 +411,8 @@
         for cp in c_dgb:
             cp.wait()
         total = dgb_all[0] + dgb_all[1] + dgb_all[2] + dgb_all[3]
-        dg_ref[...] = total[0:1].reshape(C)
-        db_ref[...] = total[1:2].reshape(C)
+        dg_ref[...] = total[:, :C].reshape(C)
+        db_ref[...] = total[:, C:].reshape(C)
     with jax.named_scope("wait_wqk"):
         l_wqk.wait()
         x_wqk.wait()
@@ -375,7 +421,13 @@
 
 def write_out(*refs):
     ins, outs, sem = refs[:7], refs[7:14], refs[14]
-    copies = [pltpu.make_async_copy(ins[i], outs[i], sem.at[i]) for i in range(7)]
+    pairs = []
+    for i in range(2):
+        for j in range(PIECES):
+            rows = pl.ds(j * (TOK // PIECES), TOK // PIECES)
+            pairs.append((ins[i].at[rows, :], outs[i].at[rows, :]))
+    pairs += [(ins[i], outs[i]) for i in range(2, 7)]
+    copies = [pltpu.make_async_copy(src, dst, sem.at[i]) for i, (src, dst) in enumerate(pairs)]
     for cp in copies:
         cp.start()
     for cp in copies:
@@ -398,7 +450,7 @@
     pk_a = vm((PK, LANES), F32)
     fold = vm((C, LANES), F32)
     scratch = [
-        rows_bf, rows_bf, vm((C,), F32), vm((C,), F32), vm((C, 3 * C), BF16), vm((C, C), BF16),
+        rows_bf, rows_bf, vm((C,), F32), vm((C,), F32), vm((C, 3 * C), BF16), vm((C, C), BF16), vm((C, C), BF16),
         pltpu.SMEM((HEADS,), F32), rows_bf, cols_bf, vm((TOK, C), F32), vm((TOK, LANES), F32),
         rows_bf, rows_bf, rows_bf, rows_bf, rows_bf, cols_bf, vm((TOK, 3 * C), BF16), rows_bf,
         win_f, win_f, vm((8, 2 * C), F32), pk_g, pk_g, pk_g, pk_g, pk_a, pk_a, pk_a, pk_a,
@@ -407,8 +459,8 @@
         vm((2, OWN, C), F32), vm((2, OWN, C), F32), vm((2, OWN, 2 * C), F32),
         vm((OWN, C), F32), vm((OWN, C), F32), vm((OWN, 2 * C), F32),
         vm((OWN, C), F32), vm((OWN, C), F32), vm((OWN, 2 * C), F32),
-        vm((4, 8, C), F32),
-        pltpu.SemaphoreType.DMA((12,)),
+        vm((4, 1, 2 * C), F32),
+        pltpu.SemaphoreType.DMA((16,)),
         pltpu.SemaphoreType.DMA((16,)), pltpu.SemaphoreType.DMA((16,)),
     ]
     parts = pl.pallas_call(
@@ -427,7 +479,7 @@
         out_shape=tuple(jax.ShapeDtypeStruct(shape, dtype) for shape, dtype in results),
         in_specs=[vmem_spec] * 7,
         out_specs=[hbm_spec] * 7,
-        scratch_shapes=[pltpu.SemaphoreType.DMA((7,))],
+        scratch_shapes=[pltpu.SemaphoreType.DMA((2 * PIECES + 5,))],
         compiler_params=pltpu.CompilerParams(vmem_limit_bytes=1024 * 1024),
     )(*parts)
 

time: 33.8 us -> 31.1 us (0.920)
  Pallas kernels: 32.9 us -> 30.2 us
    pallas_call x1, Pallas kernels: 31.1 us -> 28.3 us  [xca_local(): pl.pallas_call(kernel, name='xca', out_shape=tuple((pltpu.VMEM(shape, dty...]
where the time goes in v2:
time: 31.1 us; the launch traced here: 31 us
  Pallas kernels  30.2 us (97%)
  between operations  0.8 us (3%)
    pallas_call x1, Pallas kernels, xca_local(): pl.pallas_call(kernel, name='xca', out_shape=tuple((pltpu.VMEM(shape, dty...  28.3 us
    pallas_call x1, Pallas kernels, xca_local(): pl.pallas_call(write_out, name='xca_out', out_shape=tuple((jax.ShapeDtype...  1.86 us

profile of v2, /device:TPU:0, one launch (start us, length us, event | category | flops | bytes accessed | tf_op | source)
XLA Modules:
  0.0 31.0 jit_solution(7558451362730345547)
XLA Ops:
  0.6 28.3 %xca.1 = (bf16[2048,384]{1,0:T(8,128)(2,1)S(1)}, bf16[2048,384]{1,0:T(8,128)(2,1)S(1)}, bf16[96,1152]{1,0:T(8,128)(2,1)S(1)}, bf16[96,384]{1,0:T(8,128)(2,1)S(1)...) custom-call(bf16[2048,384]{1,0:T(8,128)(2,1)} %x_hbm.1, bf16[2048,384]{1,0:T(8,128)(2,1)} %dy_hbm.1, f32[384]{0:T(512)} %g_hbm.1, ...), custom_call_target="tpu_custom_call" | custom-call | tf_op jit(solution)/shard_map/xca/pallas_call | solution.py:466
  29.0 1.9 %xca_out.1 = (bf16[2048,384]{1,0:T(8,128)(2,1)}, bf16[2048,384]{1,0:T(8,128)(2,1)}, bf16[96,1152]{1,0:T(8,128)(2,1)}, bf16[96,384]{1,0:T(8,128)(2,1)}, f32[384]{0:T(512)}, /*index=5*/f32[384]{0:T(512)}, f32[8]{0:T(128)}) custom-call(bf16[2048,384]{1,0:T(8,128)(2,1)S(1)} %get-tuple-element.14.refs_0_, bf16[2048,384]{1,0:T(8,128)(2,1)S(1)} %get-tuple-element.15.refs_1_, ...), custom_call_target="tpu_custom_call" | custom-call | tf_op jit(solution)/shard_map/xca_out/pallas_call | solution.py:476

commit v3 on v2

--- a/solution.py
+++ b/solution.py
@@ -15,15 +15,17 @@
 TOK = 2048
 RB = 512
 NB = TOK // RB
-RA = 512
-NA = TOK // RA
+A_BLOCKS = (512, 512, 512, 512)
+NA = len(A_BLOCKS)
 RV = 256
 NV = TOK // RV
-CUT = 3
-PIECES = 4
+CUT = 4
+LAG = 3
+PIECES = 1
 SB = 64
 OWN = C // 4
 PK = 144
+HALF = PK // 2
 W0_HEADS = 5
 
 NN = (((1,), (0,)), ((), ()))
@@ -33,6 +35,10 @@
 
 def mm(a, b, dims=NN):
     return lax.dot_general(a, b, dims, preferred_element_type=F32)
+
+
+def a_block(i):
+    return sum(A_BLOCKS[:i]), A_BLOCKS[i]
 
 
 def head_rel():
@@ -75,14 +81,32 @@
     for g in range(3):
         acc = put(put(jnp.zeros((HD, LANES), F32), 2 * g, None), 2 * g + 1, None)
         spare = spare_lanes(g)
-        out_ref[pl.ds(HD * g, HD), :] = put(put(acc, 6, spare), 7, spare)
+        put_rows(out_ref, g, put(put(acc, 6, spare), 7, spare))
+
+
+def put_rows(ref, g, value):
+    if len(ref.shape) == 2:
+        ref[pl.ds(HD * g, HD), :] = value
+    elif g == 1:
+        ref[0, pl.ds(HD, HALF - HD), :] = value[: HALF - HD]
+        ref[1, pl.ds(0, HALF - HD), :] = value[HALF - HD :]
+    else:
+        ref[g // 2, pl.ds((HALF - HD) * (g // 2), HD), :] = value
+
+
+def get_rows(ref, g):
+    if len(ref.shape) == 2:
+        return ref[pl.ds(HD * g, HD), :]
+    if g == 1:
+        return jnp.concatenate([ref[0, pl.ds(HD, HALF - HD), :], ref[1, pl.ds(0, HALF - HD), :]], axis=0)
+    return ref[g // 2, pl.ds((HALF - HD) * (g // 2), HD), :]
 
 
 def packed_head(ref, h):
     if h < 6:
-        return ref[pl.ds(HD * (h // 2), HD), :]
+        return get_rows(ref, h // 2)
     lane = lax.broadcasted_iota(jnp.int32, (HD, LANES), 1)
-    return jnp.where(lane >= 96, ref[pl.ds(0, HD), :], jnp.where(lane >= 64, ref[pl.ds(HD, HD), :], ref[pl.ds(2 * HD, HD), :]))
+    return jnp.where(lane >= 96, get_rows(ref, 0), jnp.where(lane >= 64, get_rows(ref, 1), get_rows(ref, 2)))
 
 
 def spread_head(value, rels, h, win_refs):
@@ -106,9 +130,10 @@
     x_hbm, dy_hbm, g_hbm, b_hbm, wqkv_hbm, wo_hbm, tau_hbm,
     y, dx, dwqkv_ref, dwo_ref, dg_ref, db_ref, dt_ref,
     x, dy, g_ref, b_ref, wqkv, wo, wot, tau_ref, u, ut, xhat, istd, q, k, v, do, o, ot, dqkv, du,
-    g0, g1, sq, pg, rg1, sg, rg2, pa, ra1, sa, ra2,
+    g0, g1, sq, pg, rg1, sg, rg2, pa, ra1, sa,
     a0, a1, e0, e1, attn, score, qk_inv, gfull, dsq,
-    wo_part, wv_part, wqk_part, wo_r1, wv_r1, wqk_r1, wo_s, wv_s, wqk_s, wo_r2, wv_r2, wqk_r2,
+    wo_part, wv_part, wq_part, wk_part, wo_r1, wv_r1, wq_r1, wk_r1,
+    wo_s, wv_s, wq_s, wk_s, wo_r2, wv_r2, wq_r2, wk_r2,
     dgb_all,
     in_sem, send_sem, recv_sem,
 ):
@@ -131,9 +156,9 @@
         return pl.ds(i * RB, RB)
 
     ld_gb = [load(g_hbm, g_ref), load(b_hbm, b_ref)]
-    ld_x = [load(x_hbm.at[pl.ds(0, RA), :], x.at[pl.ds(0, RA), :])]
+    ld_x = [load(x_hbm.at[pl.ds(*a_block(0)), :], x.at[pl.ds(*a_block(0)), :])]
     ld_wqk = load(wqkv_hbm.at[:, pl.ds(0, 2 * C)], wqkv.at[:, pl.ds(0, 2 * C)])
-    ld_x += [load(x_hbm.at[pl.ds(i * RA, RA), :], x.at[pl.ds(i * RA, RA), :]) for i in range(1, NA)]
+    ld_x += [load(x_hbm.at[pl.ds(*a_block(i)), :], x.at[pl.ds(*a_block(i)), :]) for i in range(1, NA)]
     ld_wo = load(wo_hbm, wo)
     ld_wv = load(wqkv_hbm.at[:, pl.ds(2 * C, C)], wqkv.at[:, pl.ds(2 * C, C)])
     ld_dy = load(dy_hbm, dy)
@@ -157,8 +182,9 @@
     def step_ln(i):
         gamma = g_ref[...].reshape(1, C)
         beta = b_ref[...].reshape(1, C)
-        for j in range(RA // SB):
-            rows = pl.ds(i * RA + j * SB, SB)
+        lo, size = a_block(i)
+        for j in range(size // SB):
+            rows = pl.ds(lo + j * SB, SB)
             xf = x[rows, :].astype(F32)
             cen = xf - jnp.mean(xf, axis=-1, keepdims=True)
             inv = lax.rsqrt(jnp.mean(cen * cen, axis=-1, keepdims=True) + LN_EPS)
@@ -168,13 +194,15 @@
             u[rows, :] = (xh * gamma + beta).astype(BF16)
 
     def step_qk(i):
-        rows = pl.ds(i * RA, RA)
+        lo, size = a_block(i)
+        rows = pl.ds(lo, size)
         qk = mm(u[rows, :], wqkv[:, : 2 * C]).astype(BF16)
         q[rows, :] = qk[:, :C]
         k[rows, :] = qk[:, C:]
 
     def step_gram(i):
-        rows = pl.ds(i * RA, RA)
+        lo, size = a_block(i)
+        rows = pl.ds(lo, size)
         p0 = mm(q[rows, :256], k[rows, :256], TN)
         p1 = mm(q[rows, 128:], k[rows, 128:], TN)
         if i == 0:
@@ -184,8 +212,8 @@
             g1[...] += p1
         for r, c0 in ((q, 0), (k, C)):
             part = jnp.zeros((8, C), F32)
-            for j in range(RA // SB):
-                f = r[pl.ds(i * RA + j * SB, SB), :].astype(F32)
+            for j in range(size // SB):
+                f = r[pl.ds(lo + j * SB, SB), :].astype(F32)
                 part += jnp.sum((f * f).reshape(SB // 8, 8, C), axis=0)
             if i == 0:
                 sq[:, pl.ds(c0, C)] = part
@@ -240,28 +268,26 @@
         ld_wv.wait()
         ld_dy.wait()
         ld_tau.wait()
-        for i in range(CUT + 1):
-            if i < CUT:
-                step_b(i)
-            if i >= 1:
-                step_da(i - 1)
+        for i in range(CUT):
+            step_b(i)
     with jax.named_scope("sum_g"):
         s_g1.wait()
         sg[...] = pg[...] + rg1[...]
         s_g2 = send(sg, rg2, nbr)
     with jax.named_scope("v_do_2"):
-        for i in range(CUT, NV + 1):
-            if i < NV:
-                step_b(i)
-            if i >= CUT + 1:
-                step_da(i - 1)
+        for i in range(CUT, NV):
+            step_b(i)
+            for j in range(max(0, i - LAG) if i > CUT else 0, i + 1 - LAG):
+                step_da(j)
+        for i in range(NV - LAG, NV):
+            step_da(i)
     with jax.named_scope("fold_a"):
         fold_windows((g0, g1), pa)
-        s_a1 = send(pa, ra1, sib)
-    with jax.named_scope("sum_a"):
-        s_a1.wait()
-        sa[...] = pa[...] + ra1[...]
-        s_a2 = send(sa, ra2, nbr)
+        s_a1 = [
+            send(pa.at[1 - core], ra1.at[me], sib),
+            send(pa.at[core], ra1.at[me], nbr),
+            send(pa.at[1 - core], ra1.at[me], diag),
+        ]
 
     with jax.named_scope("wait_g"):
         s_g2.wait()
@@ -281,12 +307,14 @@
                 mask = seg_mask(rel, h, m)
                 s_q = jnp.where(mask, gfull[pl.ds(PK + m, 1), :], s_q)
                 s_k = jnp.where(mask, gfull[pl.ds(PK + 3 + m, 1), :], s_k)
-            s_q = jnp.sum(jnp.where(rel == row, s_q, 0.0), axis=1, keepdims=True)
-            inv = jnp.where(valid, lax.rsqrt(s_q) * lax.rsqrt(s_k), 0.0)
-            gram = jnp.where(valid, packed_head(gfull, h), 0.0)
-            sc = tau * gram * inv
-            top = jnp.max(jnp.where(valid, sc, -jnp.inf), axis=1, keepdims=True)
-            ex = jnp.where(valid, jnp.exp(sc - top), 0.0)
+            q_inv = lax.rsqrt(jnp.sum(jnp.where(rel == row, s_q, 0.0), axis=1, keepdims=True))
+            k_inv = lax.rsqrt(s_k)
+            by_k = packed_head(gfull, h) * k_inv
+            top = jnp.max(jnp.where(valid, by_k, -jnp.inf), axis=1, keepdims=True)
+            scale = tau * q_inv
+            sc = jnp.where(valid, scale * by_k, 0.0)
+            inv = jnp.where(valid, q_inv * k_inv, 0.0)
+            ex = jnp.where(valid, jnp.exp(sc - scale * top), 0.0)
             at = ex / jnp.sum(ex, axis=1, keepdims=True)
             hr = pl.ds(HD * h, HD)
             score[hr, :] = sc
@@ -313,6 +341,12 @@
             rows = block(i)
             dqkv[rows, 2 * C :] = window_mm(do[rows, :], (a0, a1), NN).astype(BF16)
         f_wv = part_rows(ut, far, dqkv[:, 2 * C :], wv_part, wv_r1, 0)
+    with jax.named_scope("sum_a"):
+        ra1[me] = pa[core]
+        for cp in s_a1:
+            cp.wait()
+        sa[core] = (ra1[0] + ra1[1]) + (ra1[2] + ra1[3])
+        s_a2 = send(sa.at[core], sa.at[core], sib)
     with jax.named_scope("o"):
         for i in range(NB):
             rows = block(i)
@@ -334,7 +368,7 @@
             valid = rel < HD
             hr = pl.ds(HD * h, HD)
             at = attn[hr, :]
-            d_at = jnp.where(valid, packed_head(sa, h) + packed_head(ra2, h), 0.0).astype(BF16).astype(F32)
+            d_at = jnp.where(valid, packed_head(sa, h), 0.0).astype(BF16).astype(F32)
             d_sc = at * (d_at - jnp.sum(d_at * at, axis=1, keepdims=True))
             d_sc_inv = d_sc * qk_inv[hr, :]
             d_tau_h = jnp.sum(d_sc_inv * jnp.where(valid, packed_head(gfull, h), 0.0), axis=0, keepdims=True)
@@ -350,9 +384,6 @@
         dt_ref[...] = d_tau[:, :HEADS].reshape(HEADS)
         for m in range(6):
             dsq[:, pl.ds(LANES * m, LANES)] = -dsum[m] / gfull[pl.ds(PK + m, 1), :]
-    with jax.named_scope("cross_wo"):
-        x_wo = cross(f_wo, wo_part, wo_r1, wo_s, wo_r2)
-
     with jax.named_scope("dqk"):
         for i in range(NB):
             rows = block(i)
@@ -360,15 +391,23 @@
                 window_mm(k[rows, :], (e0, e1), NT) + q[rows, :].astype(F32) * dsq[:, :C]).astype(BF16)
             dqkv[rows, C : 2 * C] = (
                 window_mm(q[rows, :], (e0, e1), NN) + k[rows, :].astype(F32) * dsq[:, C:]).astype(BF16)
-    with jax.named_scope("dwqk_far"):
-        f_wqk = part_rows(ut, far, dqkv[:, : 2 * C], wqk_part, wqk_r1, 0)
-    with jax.named_scope("near"):
+    with jax.named_scope("cross_wo"):
+        x_wo = cross(f_wo, wo_part, wo_r1, wo_s, wo_r2)
+    with jax.named_scope("dwq_far"):
+        f_wq = part_rows(ut, far, dqkv[:, :C], wq_part, wq_r1, 0)
+    with jax.named_scope("dwk_far"):
+        f_wk = part_rows(ut, far, dqkv[:, C : 2 * C], wk_part, wk_r1, 0)
+    with jax.named_scope("near_v"):
         l_wv = part_rows(ut, near, dqkv[:, 2 * C :], wv_part, wv_r1, 1)
-    with jax.named_scope("cross_wqk"):
-        x_wqk = cross(f_wqk, wqk_part, wqk_r1, wqk_s, wqk_r2)
+    with jax.named_scope("cross_wq"):
+        x_wq = cross(f_wq, wq_part, wq_r1, wq_s, wq_r2)
+    with jax.named_scope("near_o"):
+        l_wo = part_rows(ot, near, dy[...], wo_part, wo_r1, 1)
+    with jax.named_scope("cross_wk"):
+        x_wk = cross(f_wk, wk_part, wk_r1, wk_s, wk_r2)
     with jax.named_scope("near_qk"):
-        l_wo = part_rows(ot, near, dy[...], wo_part, wo_r1, 1)
-        l_wqk = part_rows(ut, near, dqkv[:, : 2 * C], wqk_part, wqk_r1, 1)
+        l_wq = part_rows(ut, near, dqkv[:, :C], wq_part, wq_r1, 1)
+        l_wk = part_rows(ut, near, dqkv[:, C : 2 * C], wk_part, wk_r1, 1)
 
     gamma = g_ref[...].reshape(1, C)
     dgam = jnp.zeros((8, C), F32)
@@ -407,6 +446,10 @@
         l_wv.wait()
         x_wv.wait()
         dwqkv_ref[:, 2 * C :] = (wv_part[1, mine, :] + wv_r1[1] + wv_r2[...]).astype(BF16)
+    with jax.named_scope("wait_wq"):
+        l_wq.wait()
+        x_wq.wait()
+        dwqkv_ref[:, :C] = (wq_part[1, mine, :] + wq_r1[1] + wq_r2[...]).astype(BF16)
     with jax.named_scope("wait_dgb"):
         for cp in c_dgb:
             cp.wait()
@@ -414,9 +457,9 @@
         dg_ref[...] = total[:, :C].reshape(C)
         db_ref[...] = total[:, C:].reshape(C)
     with jax.named_scope("wait_wqk"):
-        l_wqk.wait()
-        x_wqk.wait()
-        dwqkv_ref[:, : 2 * C] = (wqk_part[1, mine, :] + wqk_r1[1] + wqk_r2[...]).astype(BF16)
+        l_wk.wait()
+        x_wk.wait()
+        dwqkv_ref[:, C : 2 * C] = (wk_part[1, mine, :] + wk_r1[1] + wk_r2[...]).astype(BF16)
 
 
 def write_out(*refs):
@@ -447,21 +490,18 @@
     win_f = vm((256, 256), F32)
     win_b = vm((256, 256), BF16)
     pk_g = vm((PK + 8, LANES), F32)
-    pk_a = vm((PK, LANES), F32)
+    pk_a = vm((2, HALF, LANES), F32)
     fold = vm((C, LANES), F32)
     scratch = [
         rows_bf, rows_bf, vm((C,), F32), vm((C,), F32), vm((C, 3 * C), BF16), vm((C, C), BF16), vm((C, C), BF16),
         pltpu.SMEM((HEADS,), F32), rows_bf, cols_bf, vm((TOK, C), F32), vm((TOK, LANES), F32),
         rows_bf, rows_bf, rows_bf, rows_bf, rows_bf, cols_bf, vm((TOK, 3 * C), BF16), rows_bf,
-        win_f, win_f, vm((8, 2 * C), F32), pk_g, pk_g, pk_g, pk_g, pk_a, pk_a, pk_a, pk_a,
+        win_f, win_f, vm((8, 2 * C), F32), pk_g, pk_g, pk_g, pk_g, pk_a, vm((4, HALF, LANES), F32), pk_a,
         win_b, win_b, win_b, win_b, fold, fold, fold, pk_g, vm((1, 2 * C), F32),
-        vm((2, 2 * OWN, C), F32), vm((2, 2 * OWN, C), F32), vm((2, 2 * OWN, 2 * C), F32),
-        vm((2, OWN, C), F32), vm((2, OWN, C), F32), vm((2, OWN, 2 * C), F32),
-        vm((OWN, C), F32), vm((OWN, C), F32), vm((OWN, 2 * C), F32),
-        vm((OWN, C), F32), vm((OWN, C), F32), vm((OWN, 2 * C), F32),
+        *[vm((2, 2 * OWN, C), F32)] * 4, *[vm((2, OWN, C), F32)] * 4, *[vm((OWN, C), F32)] * 8,
         vm((4, 1, 2 * C), F32),
         pltpu.SemaphoreType.DMA((16,)),
-        pltpu.SemaphoreType.DMA((16,)), pltpu.SemaphoreType.DMA((16,)),
+        pltpu.SemaphoreType.DMA((24,)), pltpu.SemaphoreType.DMA((24,)),
     ]
     parts = pl.pallas_call(
         kernel,

time: 31.1 us -> 30.5 us (0.981)
  Pallas kernels: 30.2 us -> 29.6 us
    pallas_call x1, Pallas kernels: 28.3 us -> 27.8 us  [xca_local(): pl.pallas_call(kernel, name='xca', out_shape=tuple((pltpu.VMEM(shape, dty...]
where the time goes in v3:
time: 30.5 us; the launch traced here: 30.4 us
  Pallas kernels  29.6 us (97%)
  between operations  0.8 us (3%)
    pallas_call x1, Pallas kernels, xca_local(): pl.pallas_call(kernel, name='xca', out_shape=tuple((pltpu.VMEM(shape, dty...  27.8 us
    pallas_call x1, Pallas kernels, xca_local(): pl.pallas_call(write_out, name='xca_out', out_shape=tuple((jax.ShapeDtype...  1.81 us

profile of v3, /device:TPU:0, one launch (start us, length us, event | category | flops | bytes accessed | tf_op | source)
XLA Modules:
  0.0 30.4 jit_solution(14247757106577528009)
XLA Ops:
  0.6 27.8 %xca.1 = (bf16[2048,384]{1,0:T(8,128)(2,1)S(1)}, bf16[2048,384]{1,0:T(8,128)(2,1)S(1)}, bf16[96,1152]{1,0:T(8,128)(2,1)S(1)}, bf16[96,384]{1,0:T(8,128)(2,1)S(1)...) custom-call(bf16[2048,384]{1,0:T(8,128)(2,1)} %x_hbm.1, bf16[2048,384]{1,0:T(8,128)(2,1)} %dy_hbm.1, f32[384]{0:T(512)} %g_hbm.1, ...), custom_call_target="tpu_custom_call" | custom-call | tf_op jit(solution)/shard_map/xca/pallas_call | solution.py:506
  28.4 1.8 %xca_out.1 = (bf16[2048,384]{1,0:T(8,128)(2,1)}, bf16[2048,384]{1,0:T(8,128)(2,1)}, bf16[96,1152]{1,0:T(8,128)(2,1)}, bf16[96,384]{1,0:T(8,128)(2,1)}, f32[384]{0:T(512)}, /*index=5*/f32[384]{0:T(512)}, f32[8]{0:T(128)}) custom-call(bf16[2048,384]{1,0:T(8,128)(2,1)S(1)} %get-tuple-element.14.refs_0_, bf16[2048,384]{1,0:T(8,128)(2,1)S(1)} %get-tuple-element.15.refs_1_, ...), custom_call_target="tpu_custom_call" | custom-call | tf_op jit(solution)/shard_map/xca_out/pallas_call | solution.py:516

commit v4 on v3

--- a/solution.py
+++ b/solution.py
@@ -21,10 +21,12 @@
 NV = TOK // RV
 CUT = 4
 LAG = 3
+N_SENDS = 23
 PIECES = 1
 SB = 64
 OWN = C // 4
 PK = 144
+DIRECT = 16
 HALF = PK // 2
 W0_HEADS = 5
 
@@ -133,7 +135,7 @@
     g0, g1, sq, pg, rg1, sg, rg2, pa, ra1, sa,
     a0, a1, e0, e1, attn, score, qk_inv, gfull, dsq,
     wo_part, wv_part, wq_part, wk_part, wo_r1, wv_r1, wq_r1, wk_r1,
-    wo_s, wv_s, wq_s, wk_s, wo_r2, wv_r2, wq_r2, wk_r2,
+    wo_s, wv_s, wq_s, wk_s, wo_r2, wv_r2, wq_r2, wk_r2, wv_d,
     dgb_all,
     in_sem, send_sem, recv_sem,
 ):
@@ -168,15 +170,15 @@
     for peer in (sib, nbr, diag):
         pl.semaphore_signal(barrier, inc=1, device_id={"sp": peer}, device_id_type=MESH)
 
-    n_sends = [0]
+    sends = []
 
     def send(src, dst, peer):
-        i = n_sends[0]
-        n_sends[0] += 1
+        i = len(sends)
         cp = pltpu.make_async_remote_copy(
             src_ref=src, dst_ref=dst, send_sem=send_sem.at[i], recv_sem=recv_sem.at[i],
             device_id={"sp": peer}, device_id_type=MESH)
         cp.start()
+        sends.append(cp)
         return cp
 
     def step_ln(i):
@@ -229,9 +231,7 @@
     ld_wqk.wait()
     for cp in ld_x[1:]:
         cp.wait()
-    ld_wo.wait()
     with jax.named_scope("ln_qk"):
-        wot[...] = wo[...].T
         for i in range(1, NA + 2):
             if i < NA:
                 step_ln(i)
@@ -265,15 +265,27 @@
             g1[...] += p1
 
     with jax.named_scope("v_do_1"):
+        ld_wo.wait()
         ld_wv.wait()
         ld_dy.wait()
         ld_tau.wait()
+        wot[...] = wo[...].T
         for i in range(CUT):
             step_b(i)
     with jax.named_scope("sum_g"):
-        s_g1.wait()
+        s_g1.wait_recv()
         sg[...] = pg[...] + rg1[...]
-        s_g2 = send(sg, rg2, nbr)
+        s_g2 = [
+            pltpu.make_async_remote_copy(
+                src_ref=sg, dst_ref=rg2, send_sem=send_sem.at[N_SENDS + j], recv_sem=recv_sem.at[N_SENDS],
+                device_id={"sp": peer}, device_id_type=MESH)
+            for j, peer in enumerate((diag, nbr))
+        ]
+
+        @pl.when(core == 1)
+        def _():
+            for cp in s_g2:
+                cp.start()
     with jax.named_scope("v_do_2"):
         for i in range(CUT, NV):
             step_b(i)
@@ -290,7 +302,7 @@
         ]
 
     with jax.named_scope("wait_g"):
-        s_g2.wait()
+        s_g2[0].wait_recv()
     rels = head_rel()
     row = lax.broadcasted_iota(jnp.int32, (HD, LANES), 0)
     with jax.named_scope("softmax"):
@@ -324,41 +336,52 @@
 
     far = pl.ds(pl.multiple_of(2 * OWN * (1 - chip), 16), 2 * OWN)
     near = pl.ds(pl.multiple_of(2 * OWN * chip, 16), 2 * OWN)
-    theirs = pl.ds(pl.multiple_of(OWN * (1 - core), 8), OWN)
     mine = pl.ds(pl.multiple_of(OWN * core, 8), OWN)
 
-    def part_rows(lhs_t, rows, rhs, part, r1, slot):
+    def part_rows(lhs_t, rows, rhs, part, r1, slot, count=OWN):
         part[slot] = mm(lhs_t[rows, :], rhs)
-        return send(part.at[slot, theirs, :], r1.at[slot], sib)
-
-    def cross(cp, part, r1, s, r2):
-        cp.wait()
-        s[...] = part[0, mine, :] + r1[0]
-        return send(s, r2, nbr)
+        theirs = pl.ds(pl.multiple_of(OWN * (1 - core), 8), count)
+        return send(part.at[slot, theirs, :], r1.at[slot, pl.ds(0, count), :], sib)
+
+    def cross(cp, part, r1, s, r2, count=OWN):
+        cp.wait_recv()
+        rows = pl.ds(0, count)
+        s[rows, :] = part[0, pl.ds(pl.multiple_of(OWN * core, 8), count), :] + r1[0, rows, :]
+        return send(s.at[rows, :], r2.at[rows, :], nbr)
 
     with jax.named_scope("dv"):
         for i in range(NB):
             rows = block(i)
             dqkv[rows, 2 * C :] = window_mm(do[rows, :], (a0, a1), NN).astype(BF16)
-        f_wv = part_rows(ut, far, dqkv[:, 2 * C :], wv_part, wv_r1, 0)
+        f_wv = part_rows(ut, far, dqkv[:, 2 * C :], wv_part, wv_r1, 0, OWN - DIRECT)
+        d_wv = [
+            send(wv_part.at[0, pl.ds(pl.multiple_of(OWN * c + OWN - DIRECT, 8), DIRECT), :], wv_d.at[j], peer)
+            for j, (c, peer) in enumerate(((1 - core, diag), (core, nbr)))
+        ]
+    def step_o(i):
+        rows = block(i)
+        o[rows, :] = window_mm(v[rows, :], (a0, a1), NT).astype(BF16)
+        ot[:, rows] = o[rows, :].T
+
+    with jax.named_scope("o_1"):
+        for i in range(NB // 2):
+            step_o(i)
     with jax.named_scope("sum_a"):
         ra1[me] = pa[core]
         for cp in s_a1:
-            cp.wait()
+            cp.wait_recv()
         sa[core] = (ra1[0] + ra1[1]) + (ra1[2] + ra1[3])
         s_a2 = send(sa.at[core], sa.at[core], sib)
-    with jax.named_scope("o"):
-        for i in range(NB):
-            rows = block(i)
-            o[rows, :] = window_mm(v[rows, :], (a0, a1), NT).astype(BF16)
-            ot[:, rows] = o[rows, :].T
+    with jax.named_scope("o_2"):
+        for i in range(NB // 2, NB):
+            step_o(i)
     with jax.named_scope("cross_wv"):
-        x_wv = cross(f_wv, wv_part, wv_r1, wv_s, wv_r2)
+        x_wv = cross(f_wv, wv_part, wv_r1, wv_s, wv_r2, OWN - DIRECT)
     with jax.named_scope("dwo_far"):
         f_wo = part_rows(ot, far, dy[...], wo_part, wo_r1, 0)
 
     with jax.named_scope("wait_a"):
-        s_a2.wait()
+        s_a2.wait_recv()
     with jax.named_scope("softmax_bwd"):
         dsum = [jnp.zeros((1, LANES), F32) for _ in range(6)]
         lane = lax.broadcasted_iota(jnp.int32, (1, LANES), 1)
@@ -438,28 +461,41 @@
             rows = block(i)
             y[rows, :] = (x[rows, :].astype(F32) + mm(o[rows, :], wo[...])).astype(BF16)
 
+    assert len(sends) <= N_SENDS
+    @pl.when(core == 1)
+    def _():
+        for cp in s_g2:
+            cp.wait_send()
+
     with jax.named_scope("wait_wo"):
-        l_wo.wait()
-        x_wo.wait()
+        l_wo.wait_recv()
+        x_wo.wait_recv()
         dwo_ref[...] = (wo_part[1, mine, :] + wo_r1[1] + wo_r2[...]).astype(BF16)
     with jax.named_scope("wait_wv"):
-        l_wv.wait()
-        x_wv.wait()
-        dwqkv_ref[:, 2 * C :] = (wv_part[1, mine, :] + wv_r1[1] + wv_r2[...]).astype(BF16)
+        l_wv.wait_recv()
+        x_wv.wait_recv()
+        for cp in d_wv:
+            cp.wait_recv()
+        cut = OWN - DIRECT
+        near_sum = wv_part[1, mine, :] + wv_r1[1]
+        far_sum = jnp.concatenate([wv_r2[pl.ds(0, cut), :], wv_d[0] + wv_d[1]], axis=0)
+        dwqkv_ref[:, 2 * C :] = (near_sum + far_sum).astype(BF16)
     with jax.named_scope("wait_wq"):
-        l_wq.wait()
-        x_wq.wait()
+        l_wq.wait_recv()
+        x_wq.wait_recv()
         dwqkv_ref[:, :C] = (wq_part[1, mine, :] + wq_r1[1] + wq_r2[...]).astype(BF16)
     with jax.named_scope("wait_dgb"):
         for cp in c_dgb:
-            cp.wait()
+            cp.wait_recv()
         total = dgb_all[0] + dgb_all[1] + dgb_all[2] + dgb_all[3]
         dg_ref[...] = total[:, :C].reshape(C)
         db_ref[...] = total[:, C:].reshape(C)
     with jax.named_scope("wait_wqk"):
-        l_wk.wait()
-        x_wk.wait()
+        l_wk.wait_recv()
+        x_wk.wait_recv()
         dwqkv_ref[:, C : 2 * C] = (wk_part[1, mine, :] + wk_r1[1] + wk_r2[...]).astype(BF16)
+    for cp in sends:
+        cp.wait_send()
 
 
 def write_out(*refs):
@@ -498,10 +534,10 @@
         rows_bf, rows_bf, rows_bf, rows_bf, rows_bf, cols_bf, vm((TOK, 3 * C), BF16), rows_bf,
         win_f, win_f, vm((8, 2 * C), F32), pk_g, pk_g, pk_g, pk_g, pk_a, vm((4, HALF, LANES), F32), pk_a,
         win_b, win_b, win_b, win_b, fold, fold, fold, pk_g, vm((1, 2 * C), F32),
-        *[vm((2, 2 * OWN, C), F32)] * 4, *[vm((2, OWN, C), F32)] * 4, *[vm((OWN, C), F32)] * 8,
+        *[vm((2, 2 * OWN, C), F32)] * 4, *[vm((2, OWN, C), F32)] * 4, *[vm((OWN, C), F32)] * 8, vm((2, DIRECT, C), F32),
         vm((4, 1, 2 * C), F32),
         pltpu.SemaphoreType.DMA((16,)),
-        pltpu.SemaphoreType.DMA((24,)), pltpu.SemaphoreType.DMA((24,)),
+        pltpu.SemaphoreType.DMA((N_SENDS + 2,)), pltpu.SemaphoreType.DMA((N_SENDS + 1,)),
     ]
     parts = pl.pallas_call(
         kernel,

time: 30.5 us -> 29.5 us (0.967)
  Pallas kernels: 29.6 us -> 28.6 us
    pallas_call x1, Pallas kernels: 27.8 us -> 26.8 us  [xca_local(): pl.pallas_call(kernel, name='xca', out_shape=tuple((pltpu.VMEM(shape, dty...]
where the time goes in v4:
time: 29.5 us; the launch traced here: 29.4 us
  Pallas kernels  28.6 us (97%)
  between operations  0.8 us (3%)
    pallas_call x1, Pallas kernels, xca_local(): pl.pallas_call(kernel, name='xca', out_shape=tuple((pltpu.VMEM(shape, dty...  26.8 us
    pallas_call x1, Pallas kernels, xca_local(): pl.pallas_call(write_out, name='xca_out', out_shape=tuple((jax.ShapeDtype...  1.81 us

profile of v4, /device:TPU:0, one launch (start us, length us, event | category | flops | bytes accessed | tf_op | source)
XLA Modules:
  0.0 29.4 jit_solution(1196889485976252729)
XLA Ops:
  0.6 26.8 %xca.1 = (bf16[2048,384]{1,0:T(8,128)(2,1)S(1)}, bf16[2048,384]{1,0:T(8,128)(2,1)S(1)}, bf16[96,1152]{1,0:T(8,128)(2,1)S(1)}, bf16[96,384]{1,0:T(8,128)(2,1)S(1)...) custom-call(bf16[2048,384]{1,0:T(8,128)(2,1)} %x_hbm.1, bf16[2048,384]{1,0:T(8,128)(2,1)} %dy_hbm.1, f32[384]{0:T(512)} %g_hbm.1, ...), custom_call_target="tpu_custom_call" | custom-call | tf_op jit(solution)/shard_map/xca/pallas_call | solution.py:542
  27.4 1.8 %xca_out.1 = (bf16[2048,384]{1,0:T(8,128)(2,1)}, bf16[2048,384]{1,0:T(8,128)(2,1)}, bf16[96,1152]{1,0:T(8,128)(2,1)}, bf16[96,384]{1,0:T(8,128)(2,1)}, f32[384]{0:T(512)}, /*index=5*/f32[384]{0:T(512)}, f32[8]{0:T(128)}) custom-call(bf16[2048,384]{1,0:T(8,128)(2,1)S(1)} %get-tuple-element.14.refs_0_, bf16[2048,384]{1,0:T(8,128)(2,1)S(1)} %get-tuple-element.15.refs_1_, ...), custom_call_target="tpu_custom_call" | custom-call | tf_op jit(solution)/shard_map/xca_out/pallas_call | solution.py:552

commit v5 on v4

--- a/solution.py
+++ b/solution.py
@@ -21,11 +21,11 @@
 NV = TOK // RV
 CUT = 4
 LAG = 3
-N_SENDS = 23
 PIECES = 1
 SB = 64
 OWN = C // 4
 PK = 144
+LATE = 32
 DIRECT = 16
 HALF = PK // 2
 W0_HEADS = 5
@@ -137,7 +137,7 @@
     wo_part, wv_part, wq_part, wk_part, wo_r1, wv_r1, wq_r1, wk_r1,
     wo_s, wv_s, wq_s, wk_s, wo_r2, wv_r2, wq_r2, wk_r2, wv_d,
     dgb_all,
-    in_sem, send_sem, recv_sem,
+    loc_sem, recv_sem,
 ):
     me = lax.axis_index("sp")
     core = lax.rem(me, 2)
@@ -146,40 +146,45 @@
     nbr = lax.rem(me + 2, 4)
     diag = lax.rem(sib + 2, 4)
 
-    n_loads = [0]
-
-    def load(src, dst):
-        cp = pltpu.make_async_copy(src, dst, in_sem.at[n_loads[0]])
-        n_loads[0] += 1
+    def load(src, dst, slot):
+        cp = pltpu.make_async_copy(src, dst, loc_sem.at[slot])
         cp.start()
         return cp
 
     def block(i):
         return pl.ds(i * RB, RB)
 
-    ld_gb = [load(g_hbm, g_ref), load(b_hbm, b_ref)]
-    ld_x = [load(x_hbm.at[pl.ds(*a_block(0)), :], x.at[pl.ds(*a_block(0)), :])]
-    ld_wqk = load(wqkv_hbm.at[:, pl.ds(0, 2 * C)], wqkv.at[:, pl.ds(0, 2 * C)])
-    ld_x += [load(x_hbm.at[pl.ds(*a_block(i)), :], x.at[pl.ds(*a_block(i)), :]) for i in range(1, NA)]
-    ld_wo = load(wo_hbm, wo)
-    ld_wv = load(wqkv_hbm.at[:, pl.ds(2 * C, C)], wqkv.at[:, pl.ds(2 * C, C)])
-    ld_dy = load(dy_hbm, dy)
-    ld_tau = load(tau_hbm, tau_ref)
+    n0 = A_BLOCKS[0]
+    ld_gb = [load(g_hbm, g_ref, 0), load(b_hbm, b_ref, 1)]
+    ld_x0 = load(x_hbm.at[pl.ds(0, n0), :], x.at[pl.ds(0, n0), :], 2)
+    ld_wqk = load(wqkv_hbm.at[:, pl.ds(0, 2 * C)], wqkv.at[:, pl.ds(0, 2 * C)], 3)
+    ld_x1 = load(x_hbm.at[pl.ds(n0, TOK - n0), :], x.at[pl.ds(n0, TOK - n0), :], 4)
+    ld_wo = load(wo_hbm, wo, 5)
+    ld_wv = load(wqkv_hbm.at[:, pl.ds(2 * C, C)], wqkv.at[:, pl.ds(2 * C, C)], 6)
+    ld_dy = load(dy_hbm, dy, 7)
+    ld_tau = load(tau_hbm, tau_ref, 8)
 
     barrier = pltpu.get_barrier_semaphore()
     for peer in (sib, nbr, diag):
         pl.semaphore_signal(barrier, inc=1, device_id={"sp": peer}, device_id_type=MESH)
 
-    sends = []
-
-    def send(src, dst, peer):
-        i = len(sends)
-        cp = pltpu.make_async_remote_copy(
-            src_ref=src, dst_ref=dst, send_sem=send_sem.at[i], recv_sem=recv_sem.at[i],
+    busy = {}
+
+    def remote(src, dst, peer, slot, got):
+        return pltpu.make_async_remote_copy(
+            src_ref=src, dst_ref=dst, send_sem=loc_sem.at[slot], recv_sem=recv_sem.at[got],
             device_id={"sp": peer}, device_id_type=MESH)
+
+    def send(src, dst, peer, slot, got):
+        if slot in busy:
+            busy[slot].wait_send()
+        cp = remote(src, dst, peer, slot, got)
         cp.start()
-        sends.append(cp)
+        busy[slot] = cp
         return cp
+
+    def await_bytes(ref, got):
+        remote(ref, ref, sib, 0, got).wait_recv()
 
     def step_ln(i):
         gamma = g_ref[...].reshape(1, C)
@@ -221,16 +226,14 @@
                 sq[:, pl.ds(c0, C)] = part
             else:
                 sq[:, pl.ds(c0, C)] += part
-        ut[:, rows] = u[rows, :].T
 
     with jax.named_scope("ln_0"):
-        ld_x[0].wait()
+        ld_x0.wait()
         for cp in ld_gb:
             cp.wait()
         step_ln(0)
     ld_wqk.wait()
-    for cp in ld_x[1:]:
-        cp.wait()
+    ld_x1.wait()
     with jax.named_scope("ln_qk"):
         for i in range(1, NA + 2):
             if i < NA:
@@ -247,7 +250,7 @@
         pg[pl.ds(PK + 6, 2), :] = jnp.zeros((2, LANES), F32)
     with jax.named_scope("greet"):
         pl.semaphore_wait(barrier, 3)
-    s_g1 = send(pg, rg1, sib)
+    s_g1 = send(pg, rg1, sib, 0, 0)
 
     def step_b(i):
         rows = pl.ds(i * RV, RV)
@@ -272,15 +275,12 @@
         wot[...] = wo[...].T
         for i in range(CUT):
             step_b(i)
+        for i in range(NB):
+            ut[:, block(i)] = u[block(i), :].T
     with jax.named_scope("sum_g"):
         s_g1.wait_recv()
         sg[...] = pg[...] + rg1[...]
-        s_g2 = [
-            pltpu.make_async_remote_copy(
-                src_ref=sg, dst_ref=rg2, send_sem=send_sem.at[N_SENDS + j], recv_sem=recv_sem.at[N_SENDS],
-                device_id={"sp": peer}, device_id_type=MESH)
-            for j, peer in enumerate((diag, nbr))
-        ]
+        s_g2 = [remote(sg, rg2, peer, 1 + j, 1) for j, peer in enumerate((diag, nbr))]
 
         @pl.when(core == 1)
         def _():
@@ -295,11 +295,9 @@
             step_da(i)
     with jax.named_scope("fold_a"):
         fold_windows((g0, g1), pa)
-        s_a1 = [
-            send(pa.at[1 - core], ra1.at[me], sib),
-            send(pa.at[core], ra1.at[me], nbr),
-            send(pa.at[1 - core], ra1.at[me], diag),
-        ]
+        send(pa.at[1 - core], ra1.at[me], sib, 3, 2)
+        send(pa.at[core], ra1.at[me], nbr, 4, 2)
+        send(pa.at[1 - core], ra1.at[me], diag, 5, 2)
 
     with jax.named_scope("wait_g"):
         s_g2[0].wait_recv()
@@ -338,47 +336,53 @@
     near = pl.ds(pl.multiple_of(2 * OWN * chip, 16), 2 * OWN)
     mine = pl.ds(pl.multiple_of(OWN * core, 8), OWN)
 
-    def part_rows(lhs_t, rows, rhs, part, r1, slot, count=OWN):
-        part[slot] = mm(lhs_t[rows, :], rhs)
+    def part_rows(lhs_t, rows, rhs, part, r1, half, sem, got, count=OWN):
+        part[half] = mm(lhs_t[rows, :], rhs)
         theirs = pl.ds(pl.multiple_of(OWN * (1 - core), 8), count)
-        return send(part.at[slot, theirs, :], r1.at[slot, pl.ds(0, count), :], sib)
-
-    def cross(cp, part, r1, s, r2, count=OWN):
-        cp.wait_recv()
-        rows = pl.ds(0, count)
-        s[rows, :] = part[0, pl.ds(pl.multiple_of(OWN * core, 8), count), :] + r1[0, rows, :]
-        return send(s.at[rows, :], r2.at[rows, :], nbr)
+        return send(part.at[half, theirs, :], r1.at[half, pl.ds(0, count), :], sib, sem, got)
+
+    def cross(cp, part, r1, s, r2, sem, got, count=OWN, first=0):
+        if cp is not None:
+            cp.wait_recv()
+        rows = pl.ds(first, count)
+        s[rows, :] = part[0, pl.ds(pl.multiple_of(OWN * core + first, 8), count), :] + r1[0, rows, :]
+        send(s.at[rows, :], r2.at[rows, :], nbr, sem, got)
 
     with jax.named_scope("dv"):
         for i in range(NB):
             rows = block(i)
             dqkv[rows, 2 * C :] = window_mm(do[rows, :], (a0, a1), NN).astype(BF16)
-        f_wv = part_rows(ut, far, dqkv[:, 2 * C :], wv_part, wv_r1, 0, OWN - DIRECT)
-        d_wv = [
-            send(wv_part.at[0, pl.ds(pl.multiple_of(OWN * c + OWN - DIRECT, 8), DIRECT), :], wv_d.at[j], peer)
-            for j, (c, peer) in enumerate(((1 - core, diag), (core, nbr)))
-        ]
+        f_wv = part_rows(ut, far, dqkv[:, 2 * C :], wv_part, wv_r1, 0, 0, 3, OWN - DIRECT)
+        @pl.when(core == 1)
+        def _():
+            for cp in s_g2:
+                cp.wait_send()
+
+        for j, (c, peer) in enumerate(((1 - core, diag), (core, nbr))):
+            rows = pl.ds(pl.multiple_of(OWN * c + OWN - DIRECT, 8), DIRECT)
+            send(wv_part.at[0, rows, :], wv_d.at[j], peer, 1 + j, 4)
+
     def step_o(i):
         rows = block(i)
         o[rows, :] = window_mm(v[rows, :], (a0, a1), NT).astype(BF16)
-        ot[:, rows] = o[rows, :].T
 
     with jax.named_scope("o_1"):
         for i in range(NB // 2):
             step_o(i)
     with jax.named_scope("sum_a"):
         ra1[me] = pa[core]
-        for cp in s_a1:
-            cp.wait_recv()
+        await_bytes(ra1.at[pl.ds(0, 3)], 2)
         sa[core] = (ra1[0] + ra1[1]) + (ra1[2] + ra1[3])
-        s_a2 = send(sa.at[core], sa.at[core], sib)
+        s_a2 = send(sa.at[core], sa.at[core], sib, 3, 5)
     with jax.named_scope("o_2"):
         for i in range(NB // 2, NB):
             step_o(i)
     with jax.named_scope("cross_wv"):
-        x_wv = cross(f_wv, wv_part, wv_r1, wv_s, wv_r2, OWN - DIRECT)
+        cross(f_wv, wv_part, wv_r1, wv_s, wv_r2, 6, 10, OWN - DIRECT)
     with jax.named_scope("dwo_far"):
-        f_wo = part_rows(ot, far, dy[...], wo_part, wo_r1, 0)
+        for i in range(NB):
+            ot[:, block(i)] = o[block(i), :].T
+        f_wo = part_rows(ot, far, dy[...], wo_part, wo_r1, 0, 0, 6)
 
     with jax.named_scope("wait_a"):
         s_a2.wait_recv()
@@ -415,22 +419,22 @@
             dqkv[rows, C : 2 * C] = (
                 window_mm(q[rows, :], (e0, e1), NN) + k[rows, :].astype(F32) * dsq[:, C:]).astype(BF16)
     with jax.named_scope("cross_wo"):
-        x_wo = cross(f_wo, wo_part, wo_r1, wo_s, wo_r2)
+        cross(f_wo, wo_part, wo_r1, wo_s, wo_r2, 7, 10)
     with jax.named_scope("dwq_far"):
-        f_wq = part_rows(ut, far, dqkv[:, :C], wq_part, wq_r1, 0)
+        f_wq = part_rows(ut, far, dqkv[:, :C], wq_part, wq_r1, 0, 3, 7)
     with jax.named_scope("dwk_far"):
-        f_wk = part_rows(ut, far, dqkv[:, C : 2 * C], wk_part, wk_r1, 0)
+        f_wk = part_rows(ut, far, dqkv[:, C : 2 * C], wk_part, wk_r1, 0, 0, 8)
     with jax.named_scope("near_v"):
-        l_wv = part_rows(ut, near, dqkv[:, 2 * C :], wv_part, wv_r1, 1)
+        part_rows(ut, near, dqkv[:, 2 * C :], wv_part, wv_r1, 1, 8, 9)
     with jax.named_scope("cross_wq"):
-        x_wq = cross(f_wq, wq_part, wq_r1, wq_s, wq_r2)
+        cross(f_wq, wq_part, wq_r1, wq_s, wq_r2, 4, 10)
     with jax.named_scope("near_o"):
-        l_wo = part_rows(ot, near, dy[...], wo_part, wo_r1, 1)
+        part_rows(ot, near, dy[...], wo_part, wo_r1, 1, 3, 9)
     with jax.named_scope("cross_wk"):
-        x_wk = cross(f_wk, wk_part, wk_r1, wk_s, wk_r2)
+        cross(f_wk, wk_part, wk_r1, wk_s, wk_r2, 5, 11, OWN - LATE)
     with jax.named_scope("near_qk"):
-        l_wq = part_rows(ut, near, dqkv[:, :C], wq_part, wq_r1, 1)
-        l_wk = part_rows(ut, near, dqkv[:, C : 2 * C], wk_part, wk_r1, 1)
+        part_rows(ut, near, dqkv[:, :C], wq_part, wq_r1, 1, 0, 9)
+        part_rows(ut, near, dqkv[:, C : 2 * C], wk_part, wk_r1, 1, 8, 9)
 
     gamma = g_ref[...].reshape(1, C)
     dgam = jnp.zeros((8, C), F32)
@@ -455,47 +459,38 @@
                 dx[sub, :] = (dy[sub, :].astype(F32) + dln).astype(BF16)
         dgb_all[me] = jnp.concatenate(
             [jnp.sum(dgam, axis=0, keepdims=True), jnp.sum(dbet, axis=0, keepdims=True)], axis=1)
-    c_dgb = [send(dgb_all.at[me], dgb_all.at[me], peer) for peer in (sib, nbr, diag)]
+    for j, peer in enumerate((nbr, diag, sib)):
+        send(dgb_all.at[me], dgb_all.at[me], peer, 1 + j, 12)
+    cross(None, wk_part, wk_r1, wk_s, wk_r2, 6, 11, LATE, OWN - LATE)
     with jax.named_scope("y"):
         for i in range(NB):
             rows = block(i)
             y[rows, :] = (x[rows, :].astype(F32) + mm(o[rows, :], wo[...])).astype(BF16)
 
-    assert len(sends) <= N_SENDS
-    @pl.when(core == 1)
-    def _():
-        for cp in s_g2:
-            cp.wait_send()
-
-    with jax.named_scope("wait_wo"):
-        l_wo.wait_recv()
-        x_wo.wait_recv()
+    def rows_of(n):
+        return xhat.at[pl.ds(0, n), :]
+
+    with jax.named_scope("wait_wq"):
+        await_bytes(rows_of(4 * OWN), 9)
+        await_bytes(wv_d, 4)
+        await_bytes(rows_of(3 * OWN - DIRECT), 10)
         dwo_ref[...] = (wo_part[1, mine, :] + wo_r1[1] + wo_r2[...]).astype(BF16)
-    with jax.named_scope("wait_wv"):
-        l_wv.wait_recv()
-        x_wv.wait_recv()
-        for cp in d_wv:
-            cp.wait_recv()
+        dwqkv_ref[:, :C] = (wq_part[1, mine, :] + wq_r1[1] + wq_r2[...]).astype(BF16)
         cut = OWN - DIRECT
         near_sum = wv_part[1, mine, :] + wv_r1[1]
         far_sum = jnp.concatenate([wv_r2[pl.ds(0, cut), :], wv_d[0] + wv_d[1]], axis=0)
         dwqkv_ref[:, 2 * C :] = (near_sum + far_sum).astype(BF16)
-    with jax.named_scope("wait_wq"):
-        l_wq.wait_recv()
-        x_wq.wait_recv()
-        dwqkv_ref[:, :C] = (wq_part[1, mine, :] + wq_r1[1] + wq_r2[...]).astype(BF16)
     with jax.named_scope("wait_dgb"):
-        for cp in c_dgb:
-            cp.wait_recv()
+        await_bytes(dgb_all.at[pl.ds(0, 3)], 12)
         total = dgb_all[0] + dgb_all[1] + dgb_all[2] + dgb_all[3]
         dg_ref[...] = total[:, :C].reshape(C)
         db_ref[...] = total[:, C:].reshape(C)
     with jax.named_scope("wait_wqk"):
-        l_wk.wait_recv()
-        x_wk.wait_recv()
+        await_bytes(rows_of(OWN), 11)
         dwqkv_ref[:, C : 2 * C] = (wk_part[1, mine, :] + wk_r1[1] + wk_r2[...]).astype(BF16)
-    for cp in sends:
-        cp.wait_send()
+    with jax.named_scope("sends"):
+        for cp in busy.values():
+            cp.wait_send()
 
 
 def write_out(*refs):
@@ -536,8 +531,7 @@
         win_b, win_b, win_b, win_b, fold, fold, fold, pk_g, vm((1, 2 * C), F32),
         *[vm((2, 2 * OWN, C), F32)] * 4, *[vm((2, OWN, C), F32)] * 4, *[vm((OWN, C), F32)] * 8, vm((2, DIRECT, C), F32),
         vm((4, 1, 2 * C), F32),
-        pltpu.SemaphoreType.DMA((16,)),
-        pltpu.SemaphoreType.DMA((N_SENDS + 2,)), pltpu.SemaphoreType.DMA((N_SENDS + 1,)),
+        pltpu.SemaphoreType.DMA((9,)), pltpu.SemaphoreType.DMA((13,)),
     ]
     parts = pl.pallas_call(
         kernel,

time: 29.5 us -> 29 us (0.983)
  Pallas kernels: 28.6 us -> 28.1 us
    pallas_call x1, Pallas kernels: 26.8 us -> 26.3 us  [xca_local(): pl.pallas_call(kernel, name='xca', out_shape=tuple((pltpu.VMEM(shape, dty...]
where the time goes in v5:
time: 29 us; the launch traced here: 28.9 us
  Pallas kernels  28.1 us (97%)
  between operations  0.8 us (3%)
    pallas_call x1, Pallas kernels, xca_local(): pl.pallas_call(kernel, name='xca', out_shape=tuple((pltpu.VMEM(shape, dty...  26.3 us
    pallas_call x1, Pallas kernels, xca_local(): pl.pallas_call(write_out, name='xca_out', out_shape=tuple((jax.ShapeDtype...  1.81 us

profile of v5, /device:TPU:0, one launch (start us, length us, event | category | flops | bytes accessed | tf_op | source)
XLA Modules:
  0.0 28.9 jit_solution(6320909964779677697)
XLA Ops:
  0.6 26.3 %xca.1 = (bf16[2048,384]{1,0:T(8,128)(2,1)S(1)}, bf16[2048,384]{1,0:T(8,128)(2,1)S(1)}, bf16[96,1152]{1,0:T(8,128)(2,1)S(1)}, bf16[96,384]{1,0:T(8,128)(2,1)S(1)...) custom-call(bf16[2048,384]{1,0:T(8,128)(2,1)} %x_hbm.1, bf16[2048,384]{1,0:T(8,128)(2,1)} %dy_hbm.1, f32[384]{0:T(512)} %g_hbm.1, ...), custom_call_target="tpu_custom_call" | custom-call | tf_op jit(solution)/shard_map/xca/pallas_call | solution.py:536
  26.9 1.8 %xca_out.1 = (bf16[2048,384]{1,0:T(8,128)(2,1)}, bf16[2048,384]{1,0:T(8,128)(2,1)}, bf16[96,1152]{1,0:T(8,128)(2,1)}, bf16[96,384]{1,0:T(8,128)(2,1)}, f32[384]{0:T(512)}, /*index=5*/f32[384]{0:T(512)}, f32[8]{0:T(128)}) custom-call(bf16[2048,384]{1,0:T(8,128)(2,1)S(1)} %get-tuple-element.14.refs_0_, bf16[2048,384]{1,0:T(8,128)(2,1)S(1)} %get-tuple-element.15.refs_1_, ...), custom_call_target="tpu_custom_call" | custom-call | tf_op jit(solution)/shard_map/xca_out/pallas_call | solution.py:546

commit v6 on v5

--- a/solution.py
+++ b/solution.py
@@ -25,7 +25,8 @@
 SB = 64
 OWN = C // 4
 PK = 144
-LATE = 32
+LATE = 48
+MOVE = 40
 DIRECT = 16
 HALF = PK // 2
 W0_HEADS = 5
@@ -135,7 +136,7 @@
     g0, g1, sq, pg, rg1, sg, rg2, pa, ra1, sa,
     a0, a1, e0, e1, attn, score, qk_inv, gfull, dsq,
     wo_part, wv_part, wq_part, wk_part, wo_r1, wv_r1, wq_r1, wk_r1,
-    wo_s, wv_s, wq_s, wk_s, wo_r2, wv_r2, wq_r2, wk_r2, wv_d,
+    wo_s, wv_s, wq_s, wk_s, wo_r2, wv_r2, wq_r2, wk_r2, wv_d, wk_x, wk_m,
     dgb_all,
     loc_sem, recv_sem,
 ):
@@ -341,11 +342,10 @@
         theirs = pl.ds(pl.multiple_of(OWN * (1 - core), 8), count)
         return send(part.at[half, theirs, :], r1.at[half, pl.ds(0, count), :], sib, sem, got)
 
-    def cross(cp, part, r1, s, r2, sem, got, count=OWN, first=0):
-        if cp is not None:
-            cp.wait_recv()
-        rows = pl.ds(first, count)
-        s[rows, :] = part[0, pl.ds(pl.multiple_of(OWN * core + first, 8), count), :] + r1[0, rows, :]
+    def cross(cp, part, r1, s, r2, sem, got, count=OWN):
+        cp.wait_recv()
+        rows = pl.ds(0, count)
+        s[rows, :] = part[0, pl.ds(pl.multiple_of(OWN * core, 8), count), :] + r1[0, rows, :]
         send(s.at[rows, :], r2.at[rows, :], nbr, sem, got)
 
     with jax.named_scope("dv"):
@@ -424,6 +424,13 @@
         f_wq = part_rows(ut, far, dqkv[:, :C], wq_part, wq_r1, 0, 3, 7)
     with jax.named_scope("dwk_far"):
         f_wk = part_rows(ut, far, dqkv[:, C : 2 * C], wk_part, wk_r1, 0, 0, 8)
+        last = pl.ds(OWN - MOVE, MOVE)
+        hand = remote(wk_part.at[0, last, :], wk_x, sib, 9, 13)
+
+        @pl.when(core == 0)
+        def _():
+            hand.start()
+
     with jax.named_scope("near_v"):
         part_rows(ut, near, dqkv[:, 2 * C :], wv_part, wv_r1, 1, 8, 9)
     with jax.named_scope("cross_wq"):
@@ -461,7 +468,27 @@
             [jnp.sum(dgam, axis=0, keepdims=True), jnp.sum(dbet, axis=0, keepdims=True)], axis=1)
     for j, peer in enumerate((nbr, diag, sib)):
         send(dgb_all.at[me], dgb_all.at[me], peer, 1 + j, 12)
-    cross(None, wk_part, wk_r1, wk_s, wk_r2, 6, 11, LATE, OWN - LATE)
+    late = pl.ds(OWN - LATE, LATE)
+    wk_s[late, :] = wk_part[0, pl.ds(pl.multiple_of(OWN * core + OWN - LATE, 8), LATE), :] + wk_r1[0, late, :]
+    busy.pop(6).wait_send()
+
+    def late_copy(count):
+        rows = pl.ds(OWN - LATE, count)
+        return remote(wk_s.at[rows, :], wk_r2.at[rows, :], nbr, 6, 11)
+
+    moved = remote(wk_m, wk_r2.at[last, :], diag, 9, 11)
+
+    @pl.when(core == 0)
+    def _():
+        late_copy(LATE - MOVE).start()
+
+    @pl.when(core == 1)
+    def _():
+        hand.wait_recv()
+        wk_m[...] = wk_part[0, last, :] + wk_x[...]
+        moved.start()
+        late_copy(LATE).start()
+
     with jax.named_scope("y"):
         for i in range(NB):
             rows = block(i)
@@ -492,6 +519,16 @@
         for cp in busy.values():
             cp.wait_send()
 
+        @pl.when(core == 0)
+        def _():
+            hand.wait_send()
+            late_copy(LATE - MOVE).wait_send()
+
+        @pl.when(core == 1)
+        def _():
+            moved.wait_send()
+            late_copy(LATE).wait_send()
+
 
 def write_out(*refs):
     ins, outs, sem = refs[:7], refs[7:14], refs[14]
@@ -529,9 +566,9 @@
         rows_bf, rows_bf, rows_bf, rows_bf, rows_bf, cols_bf, vm((TOK, 3 * C), BF16), rows_bf,
         win_f, win_f, vm((8, 2 * C), F32), pk_g, pk_g, pk_g, pk_g, pk_a, vm((4, HALF, LANES), F32), pk_a,
         win_b, win_b, win_b, win_b, fold, fold, fold, pk_g, vm((1, 2 * C), F32),
-        *[vm((2, 2 * OWN, C), F32)] * 4, *[vm((2, OWN, C), F32)] * 4, *[vm((OWN, C), F32)] * 8, vm((2, DIRECT, C), F32),
+        *[vm((2, 2 * OWN, C), F32)] * 4, *[vm((2, OWN, C), F32)] * 4, *[vm((OWN, C), F32)] * 8, vm((2, DIRECT, C), F32), vm((MOVE, C), F32), vm((MOVE, C), F32),
         vm((4, 1, 2 * C), F32),
-        pltpu.SemaphoreType.DMA((9,)), pltpu.SemaphoreType.DMA((13,)),
+        pltpu.SemaphoreType.DMA((10,)), pltpu.SemaphoreType.DMA((14,)),
     ]
     parts = pl.pallas_call(
         kernel,

time: 29 us -> 28.2 us (0.972)
  Pallas kernels: 28.1 us -> 27.3 us
    pallas_call x1, Pallas kernels: 26.3 us -> 25.5 us  [xca_local(): pl.pallas_call(kernel, name='xca', out_shape=tuple((pltpu.VMEM(shape, dty...]
where the time goes in v6:
time: 28.2 us; the launch traced here: 28.1 us
  Pallas kernels  27.3 us (97%)
  between operations  0.8 us (3%)
    pallas_call x1, Pallas kernels, xca_local(): pl.pallas_call(kernel, name='xca', out_shape=tuple((pltpu.VMEM(shape, dty...  25.5 us
    pallas_call x1, Pallas kernels, xca_local(): pl.pallas_call(write_out, name='xca_out', out_shape=tuple((jax.ShapeDtype...  1.81 us

profile of v6, /device:TPU:0, one launch (start us, length us, event | category | flops | bytes accessed | tf_op | source)
XLA Modules:
  0.0 28.1 jit_solution(14489243788061784318)
XLA Ops:
  0.6 25.5 %xca.1 = (bf16[2048,384]{1,0:T(8,128)(2,1)S(1)}, bf16[2048,384]{1,0:T(8,128)(2,1)S(1)}, bf16[96,1152]{1,0:T(8,128)(2,1)S(1)}, bf16[96,384]{1,0:T(8,128)(2,1)S(1)...) custom-call(bf16[2048,384]{1,0:T(8,128)(2,1)} %x_hbm.1, bf16[2048,384]{1,0:T(8,128)(2,1)} %dy_hbm.1, f32[384]{0:T(512)} %g_hbm.1, ...), custom_call_target="tpu_custom_call" | custom-call | tf_op jit(solution)/shard_map/xca/pallas_call | solution.py:573
  26.2 1.8 %xca_out.1 = (bf16[2048,384]{1,0:T(8,128)(2,1)}, bf16[2048,384]{1,0:T(8,128)(2,1)}, bf16[96,1152]{1,0:T(8,128)(2,1)}, bf16[96,384]{1,0:T(8,128)(2,1)}, f32[384]{0:T(512)}, /*index=5*/f32[384]{0:T(512)}, f32[8]{0:T(128)}) custom-call(bf16[2048,384]{1,0:T(8,128)(2,1)S(1)} %get-tuple-element.14.refs_0_, bf16[2048,384]{1,0:T(8,128)(2,1)S(1)} %get-tuple-element.15.refs_1_, ...), custom_call_target="tpu_custom_call" | custom-call | tf_op jit(solution)/shard_map/xca_out/pallas_call | solution.py:583

commit v7 on v6

--- a/solution.py
+++ b/solution.py
@@ -25,8 +25,8 @@
 SB = 64
 OWN = C // 4
 PK = 144
-LATE = 48
-MOVE = 40
+LATE = 64
+MOVE = 48
 DIRECT = 16
 HALF = PK // 2
 W0_HEADS = 5
@@ -375,11 +375,12 @@
         sa[core] = (ra1[0] + ra1[1]) + (ra1[2] + ra1[3])
         s_a2 = send(sa.at[core], sa.at[core], sib, 3, 5)
     with jax.named_scope("o_2"):
-        for i in range(NB // 2, NB):
+        for i in range(NB // 2, NB - 1):
             step_o(i)
     with jax.named_scope("cross_wv"):
         cross(f_wv, wv_part, wv_r1, wv_s, wv_r2, 6, 10, OWN - DIRECT)
     with jax.named_scope("dwo_far"):
+        step_o(NB - 1)
         for i in range(NB):
             ot[:, block(i)] = o[block(i), :].T
         f_wo = part_rows(ot, far, dy[...], wo_part, wo_r1, 0, 0, 6)
@@ -439,10 +440,6 @@
         part_rows(ot, near, dy[...], wo_part, wo_r1, 1, 3, 9)
     with jax.named_scope("cross_wk"):
         cross(f_wk, wk_part, wk_r1, wk_s, wk_r2, 5, 11, OWN - LATE)
-    with jax.named_scope("near_qk"):
-        part_rows(ut, near, dqkv[:, :C], wq_part, wq_r1, 1, 0, 9)
-        part_rows(ut, near, dqkv[:, C : 2 * C], wk_part, wk_r1, 1, 8, 9)
-
     gamma = g_ref[...].reshape(1, C)
     dgam = jnp.zeros((8, C), F32)
     dbet = jnp.zeros((8, C), F32)
@@ -489,6 +486,9 @@
         moved.start()
         late_copy(LATE).start()
 
+    with jax.named_scope("near_qk"):
+        part_rows(ut, near, dqkv[:, :C], wq_part, wq_r1, 1, 0, 9)
+        part_rows(ut, near, dqkv[:, C : 2 * C], wk_part, wk_r1, 1, 8, 9)
     with jax.named_scope("y"):
         for i in range(NB):
             rows = block(i)

time: 28.2 us -> 28.2 us (level)
  no operation moved by 1% of the time
where the time goes in v7:
time: 28.2 us; the launch traced here: 27.9 us
  Pallas kernels  27.1 us (96%)
  between operations  0.8 us (3%)
    pallas_call x1, Pallas kernels, xca_local(): pl.pallas_call(kernel, name='xca', out_shape=tuple((pltpu.VMEM(shape, dty...  25.2 us
    pallas_call x1, Pallas kernels, xca_local(): pl.pallas_call(write_out, name='xca_out', out_shape=tuple((jax.ShapeDtype...  1.81 us

profile of v7, /device:TPU:0, one launch (start us, length us, event | category | flops | bytes accessed | tf_op | source)
XLA Modules:
  0.0 27.9 jit_solution(12152582817919284245)
XLA Ops:
  0.6 25.2 %xca.1 = (bf16[2048,384]{1,0:T(8,128)(2,1)S(1)}, bf16[2048,384]{1,0:T(8,128)(2,1)S(1)}, bf16[96,1152]{1,0:T(8,128)(2,1)S(1)}, bf16[96,384]{1,0:T(8,128)(2,1)S(1)...) custom-call(bf16[2048,384]{1,0:T(8,128)(2,1)} %x_hbm.1, bf16[2048,384]{1,0:T(8,128)(2,1)} %dy_hbm.1, f32[384]{0:T(512)} %g_hbm.1, ...), custom_call_target="tpu_custom_call" | custom-call | tf_op jit(solution)/shard_map/xca/pallas_call | solution.py:573
  25.9 1.8 %xca_out.1 = (bf16[2048,384]{1,0:T(8,128)(2,1)}, bf16[2048,384]{1,0:T(8,128)(2,1)}, bf16[96,1152]{1,0:T(8,128)(2,1)}, bf16[96,384]{1,0:T(8,128)(2,1)}, f32[384]{0:T(512)}, /*index=5*/f32[384]{0:T(512)}, f32[8]{0:T(128)}) custom-call(bf16[2048,384]{1,0:T(8,128)(2,1)S(1)} %get-tuple-element.14.refs_0_, bf16[2048,384]{1,0:T(8,128)(2,1)S(1)} %get-tuple-element.15.refs_1_, ...), custom_call_target="tpu_custom_call" | custom-call | tf_op jit(solution)/shard_map/xca_out/pallas_call | solution.py:583

commit v8 on v6

--- a/solution.py
+++ b/solution.py
@@ -360,7 +360,7 @@
 
         for j, (c, peer) in enumerate(((1 - core, diag), (core, nbr))):
             rows = pl.ds(pl.multiple_of(OWN * c + OWN - DIRECT, 8), DIRECT)
-            send(wv_part.at[0, rows, :], wv_d.at[j], peer, 1 + j, 4)
+            send(wv_part.at[0, rows, :], wv_d.at[j], peer, 1 + j, 9)
 
     def step_o(i):
         rows = block(i)
@@ -378,7 +378,7 @@
         for i in range(NB // 2, NB):
             step_o(i)
     with jax.named_scope("cross_wv"):
-        cross(f_wv, wv_part, wv_r1, wv_s, wv_r2, 6, 10, OWN - DIRECT)
+        cross(f_wv, wv_part, wv_r1, wv_s, wv_r2, 6, 9, OWN - DIRECT)
     with jax.named_scope("dwo_far"):
         for i in range(NB):
             ot[:, block(i)] = o[block(i), :].T
@@ -419,13 +419,13 @@
             dqkv[rows, C : 2 * C] = (
                 window_mm(q[rows, :], (e0, e1), NN) + k[rows, :].astype(F32) * dsq[:, C:]).astype(BF16)
     with jax.named_scope("cross_wo"):
-        cross(f_wo, wo_part, wo_r1, wo_s, wo_r2, 7, 10)
+        cross(f_wo, wo_part, wo_r1, wo_s, wo_r2, 7, 9)
     with jax.named_scope("dwq_far"):
         f_wq = part_rows(ut, far, dqkv[:, :C], wq_part, wq_r1, 0, 3, 7)
     with jax.named_scope("dwk_far"):
         f_wk = part_rows(ut, far, dqkv[:, C : 2 * C], wk_part, wk_r1, 0, 0, 8)
         last = pl.ds(OWN - MOVE, MOVE)
-        hand = remote(wk_part.at[0, last, :], wk_x, sib, 9, 13)
+        hand = remote(wk_part.at[0, last, :], wk_x, sib, 9, 4)
 
         @pl.when(core == 0)
         def _():
@@ -434,7 +434,7 @@
     with jax.named_scope("near_v"):
         part_rows(ut, near, dqkv[:, 2 * C :], wv_part, wv_r1, 1, 8, 9)
     with jax.named_scope("cross_wq"):
-        cross(f_wq, wq_part, wq_r1, wq_s, wq_r2, 4, 10)
+        cross(f_wq, wq_part, wq_r1, wq_s, wq_r2, 4, 9)
     with jax.named_scope("near_o"):
         part_rows(ot, near, dy[...], wo_part, wo_r1, 1, 3, 9)
     with jax.named_scope("cross_wk"):
@@ -467,7 +467,7 @@
         dgb_all[me] = jnp.concatenate(
             [jnp.sum(dgam, axis=0, keepdims=True), jnp.sum(dbet, axis=0, keepdims=True)], axis=1)
     for j, peer in enumerate((nbr, diag, sib)):
-        send(dgb_all.at[me], dgb_all.at[me], peer, 1 + j, 12)
+        send(dgb_all.at[me], dgb_all.at[me], peer, 1 + j, 10)
     late = pl.ds(OWN - LATE, LATE)
     wk_s[late, :] = wk_part[0, pl.ds(pl.multiple_of(OWN * core + OWN - LATE, 8), LATE), :] + wk_r1[0, late, :]
     busy.pop(6).wait_send()
@@ -498,9 +498,7 @@
         return xhat.at[pl.ds(0, n), :]
 
     with jax.named_scope("wait_wq"):
-        await_bytes(rows_of(4 * OWN), 9)
-        await_bytes(wv_d, 4)
-        await_bytes(rows_of(3 * OWN - DIRECT), 10)
+        await_bytes(rows_of(7 * OWN + DIRECT), 9)
         dwo_ref[...] = (wo_part[1, mine, :] + wo_r1[1] + wo_r2[...]).astype(BF16)
         dwqkv_ref[:, :C] = (wq_part[1, mine, :] + wq_r1[1] + wq_r2[...]).astype(BF16)
         cut = OWN - DIRECT
@@ -508,7 +506,7 @@
         far_sum = jnp.concatenate([wv_r2[pl.ds(0, cut), :], wv_d[0] + wv_d[1]], axis=0)
         dwqkv_ref[:, 2 * C :] = (near_sum + far_sum).astype(BF16)
     with jax.named_scope("wait_dgb"):
-        await_bytes(dgb_all.at[pl.ds(0, 3)], 12)
+        await_bytes(dgb_all.at[pl.ds(0, 3)], 10)
         total = dgb_all[0] + dgb_all[1] + dgb_all[2] + dgb_all[3]
         dg_ref[...] = total[:, :C].reshape(C)
         db_ref[...] = total[:, C:].reshape(C)
@@ -568,7 +566,7 @@
         win_b, win_b, win_b, win_b, fold, fold, fold, pk_g, vm((1, 2 * C), F32),
         *[vm((2, 2 * OWN, C), F32)] * 4, *[vm((2, OWN, C), F32)] * 4, *[vm((OWN, C), F32)] * 8, vm((2, DIRECT, C), F32), vm((MOVE, C), F32), vm((MOVE, C), F32),
         vm((4, 1, 2 * C), F32),
-        pltpu.SemaphoreType.DMA((10,)), pltpu.SemaphoreType.DMA((14,)),
+        pltpu.SemaphoreType.DMA((10,)), pltpu.SemaphoreType.DMA((12,)),
     ]
     parts = pl.pallas_call(
         kernel,

time: 28.2 us -> 28.2 us (level)
  no operation moved by 1% of the time
where the time goes in v8:
time: 28.2 us; the launch traced here: 28.1 us
  Pallas kernels  27.3 us (97%)
  between operations  0.8 us (3%)
    pallas_call x1, Pallas kernels, xca_local(): pl.pallas_call(kernel, name='xca', out_shape=tuple((pltpu.VMEM(shape, dty...  25.5 us
    pallas_call x1, Pallas kernels, xca_local(): pl.pallas_call(write_out, name='xca_out', out_shape=tuple((jax.ShapeDtype...  1.81 us

profile of v8, /device:TPU:0, one launch (start us, length us, event | category | flops | bytes accessed | tf_op | source)
XLA Modules:
  0.0 28.1 jit_solution(16208775745136081927)
XLA Ops:
  0.6 25.5 %xca.1 = (bf16[2048,384]{1,0:T(8,128)(2,1)S(1)}, bf16[2048,384]{1,0:T(8,128)(2,1)S(1)}, bf16[96,1152]{1,0:T(8,128)(2,1)S(1)}, bf16[96,384]{1,0:T(8,128)(2,1)S(1)...) custom-call(bf16[2048,384]{1,0:T(8,128)(2,1)} %x_hbm.1, bf16[2048,384]{1,0:T(8,128)(2,1)} %dy_hbm.1, f32[384]{0:T(512)} %g_hbm.1, ...), custom_call_target="tpu_custom_call" | custom-call | tf_op jit(solution)/shard_map/xca/pallas_call | solution.py:571
  26.1 1.8 %xca_out.1 = (bf16[2048,384]{1,0:T(8,128)(2,1)}, bf16[2048,384]{1,0:T(8,128)(2,1)}, bf16[96,1152]{1,0:T(8,128)(2,1)}, bf16[96,384]{1,0:T(8,128)(2,1)}, f32[384]{0:T(512)}, /*index=5*/f32[384]{0:T(512)}, f32[8]{0:T(128)}) custom-call(bf16[2048,384]{1,0:T(8,128)(2,1)S(1)} %get-tuple-element.14.refs_0_, bf16[2048,384]{1,0:T(8,128)(2,1)S(1)} %get-tuple-element.15.refs_1_, ...), custom_call_target="tpu_custom_call" | custom-call | tf_op jit(solution)/shard_map/xca_out/pallas_call | solution.py:581
